TPU v7x, 512 devices: a 8x2x16 block of a 8x8x16 slice. The times are simulated.
512 devices in a mesh: grp: 2 (over y), seq: 128 (over z, x), head: 2 (over core).
Axes of the slice: x: 8, y: 2, z: 16, core: 2. Of those that a mesh axis runs over, the one named last changes fastest.
The devices are a block of a 8x8x16 slice.
Arguments:
- queries: bfloat16 [98304, 768], P(('grp', 'seq'), 'head'), parts along dimension 0, may hold values from -6 to 6
- key_rows: bfloat16 [98304, 768], P(('grp', 'seq'), 'head'), parts along dimension 0, may hold values from -6 to 6
- value_rows: bfloat16 [98304, 768], P(('grp', 'seq'), 'head'), parts along dimension 0, may hold values from -6 to 6
- gate_input: bfloat16 [98304, 768], P(('grp', 'seq'), 'head'), parts along dimension 0, may hold values from -6 to 6
- norm_gain: float32 [768], P('head'), may hold values from 0.5 to 1.5
Outputs:
- retained: bfloat16 [98304, 768], P(('grp', 'seq'), 'head'), parts along dimension 0
- final_state: float32 [256, 6, 128], P(('grp', 'seq'), 'head'), parts along dimension 0
There are 2 independent parts, one for each index of `grp`. A program takes and returns all parts, laid end to end along the dimension named above; an argument that names none is the same for every part. Nothing has to cross between parts.
All inputs are finite; a program needn't handle non-finite values.
Results may differ from a plain program's by a relative error of at most 0.0056.
Values sent between devices are 32-bit elements; how exact they have to be, the bound alone decides.
A program may use at most 128 MiB of HBM per device.

v0:
```python
import jax
import jax.numpy as jnp
from jax import lax
from jax.sharding import Mesh
from jax.sharding import PartitionSpec as P

ALL_HEADS = 10
HEADS = 6
DH = 128
SEQ = ("seq_0", "seq_1")
GRP_SEQ = ("grp", "seq_0", "seq_1")


def filled_with(shard, identity):
    return jax.tree.map(
        lambda a, e: jnp.broadcast_to(jnp.asarray(e, a.dtype), a.shape), shard, identity
    )


def carried_in(shard, axes, combine, identity):
    before = start = filled_with(shard, identity)
    so_far = shard
    for axis in reversed(axes):
        peers, mine = (lax.axis_size(axis), lax.axis_index(axis))
        pieces = jax.tree.map(lambda part: lax.all_gather(part, axis), so_far)
        inside, so_far = (start, start)
        for k in range(peers):
            passed = k < mine
            so_far = combine(so_far, jax.tree.map(lambda part: part[k], pieces))
            inside = jax.tree.map(lambda new, old: jnp.where(passed, new, old), so_far, inside)
        before = combine(inside, before)
    return before


def scatter_axes(shard, axes, dim):
    for axis in axes:
        shard = lax.psum_scatter(shard, axis, scatter_dimension=dim, tiled=True)
    return shard


def combine(earlier, latter):
    return (earlier[0] * latter[0], latter[0][None, :, None] * earlier[1] + latter[1])


def body(queries, key_rows, value_rows, gate_input, norm_gain):
    tokens = queries.shape[0]
    local_heads = queries.shape[1] // DH
    key_scale = DH ** (-0.5)
    head_ids = (
        ALL_HEADS
        - HEADS
        + lax.axis_index("head") * local_heads
        + jnp.arange(local_heads, dtype=jnp.int32)
    ).astype(jnp.float32)
    log_decay = jnp.log1p(-jnp.exp2(-5.0 - head_ids))
    split_shape = (tokens, local_heads, DH)
    query_split = queries.reshape(split_shape)
    key_split = key_rows.reshape(split_shape)
    value_split = value_rows.reshape(split_shape)
    places = jnp.arange(tokens, dtype=jnp.float32)
    offsets = places[:, None] - places[None, :]
    causal = offsets >= 0
    decays = jnp.where(
        causal[None], jnp.exp(jnp.where(causal, offsets, 0.0)[None] * log_decay[:, None, None]), 0.0
    )
    tail_decay = jnp.exp((tokens - 1 - places)[:, None] * log_decay[None, :])
    keys_decayed = (key_split.astype(jnp.float32) * key_scale * tail_decay[:, :, None]).astype(
        jnp.bfloat16
    )
    local_state = jnp.einsum(
        "shi,shj->ihj", keys_decayed, value_split, preferred_element_type=jnp.float32
    )
    block_decay = jnp.exp(tokens * log_decay)
    identity = (jnp.ones_like(block_decay), jnp.zeros_like(local_state))
    prefix_decay, carried = carried_in((block_decay, local_state), SEQ, combine, identity)
    scores = (
        jnp.einsum("thd,shd->hts", query_split, key_split, preferred_element_type=jnp.float32)
        * key_scale
    )
    weights = (scores * decays).astype(jnp.bfloat16)
    inner_term = jnp.einsum(
        "hts,shd->thd", weights, value_split, preferred_element_type=jnp.float32
    )
    lead_decay = jnp.exp((places + 1)[:, None] * log_decay[None, :])
    outer_term = (
        jnp.einsum(
            "thi,ihj->thj",
            query_split,
            carried.astype(jnp.bfloat16),
            preferred_element_type=jnp.float32,
        )
        * lead_decay[:, :, None]
    )
    mixture = inner_term + outer_term
    centred = mixture - jnp.mean(mixture, axis=-1, keepdims=True)
    variance = jnp.mean(centred * centred, axis=-1, keepdims=True)
    normed = centred * lax.rsqrt(variance + 1e-05) * norm_gain.reshape(local_heads, DH)
    gated = normed * jax.nn.silu(gate_input.reshape(split_shape).astype(jnp.float32))
    result = gated.astype(jnp.bfloat16).reshape(tokens, local_heads * DH)
    ahead = (lax.axis_size(SEQ) - 1 - lax.axis_index(SEQ)).astype(jnp.float32)
    scaled_terms = jnp.exp(ahead * tokens * log_decay)[None, :, None] * local_state
    final_state = scatter_axes(scaled_terms, SEQ, 0)
    return (result, final_state)


def solution(mesh):
    finer = Mesh(
        mesh.devices.reshape(mesh.shape["grp"], 16, 8, mesh.shape["head"]),
        ("grp", "seq_0", "seq_1", "head"),
    )
    placed = (
        P(GRP_SEQ, "head"),
        P(GRP_SEQ, "head"),
        P(GRP_SEQ, "head"),
        P(GRP_SEQ, "head"),
        P("head"),
    )
    return jax.shard_map(
        body,
        mesh=finer,
        in_specs=placed,
        out_specs=(P(GRP_SEQ, "head"), P(GRP_SEQ, "head", None)),
        check_vma=False,
    )
```

profile of v0, /device:TPU:68, one launch (start us, length us, event | category | flops | bytes accessed | tf_op | source)
XLA Modules:
  0.0 212.4 jit_solution(16647699294125695046)
XLA Ops:
  8.1 1.2 copy.23
  9.3 1.2 copy.26
  10.5 0.1 exponential_multiply_fusion
  10.6 1.0 broadcast_multiply_fusion
  11.7 0.1 reduce-scatter.3.cloned.1.call-start
  11.8 0.6 reduce-scatter.3.cloned.1.call-update
  12.3 0.1 all-gather.6.cloned.1.call-start
  12.4 51.0 %all-gather.1 = f32[8,1,3]{2,1,0:T(1,128)S(1)} all-gather(f32[1,1,3]{2,1,0:T(1,128)S(1)} %exponential_bitcast_fusion), channel_id=1, replica_groups=mesh['grp'=2,'seq_0'=16,'seq_1'=8,'head'=2] {'seq_1'}, dimensions={0}, use_global_device_ids=true | all-gather | bytes 108 | tf_op jit(solution)/shard_map/all_gather | solution.py:25
  63.4 26.5 %all-gather.8.cloned.1.call-done = f32[1024,3,128]{2,0,1:T(8,128)} async-done(((f32[128,3,128]{2,0,1:T(8,128)}), f32[1024,3,128]{2,0,1:T(8,128)}) %all-gather.8.cloned.1.call-update) | async-done | bytes 1572880 | tf_op jit(solution)/shard_map/all_gather | solution.py:25
  89.9 2.3 %bitcast_add_fusion = f32[1,128,3,128]{3,1,2,0:T(8,128)} fusion(f32[1024,3,128]{2,0,1:T(8,128)} %all-gather.8.cloned.1.call-done, f32[3]{0:T(128)S(1)} %get-tuple-element.25, f32[3]{0:T(128)S(1)} %get-tuple-element.32, f32[3]{0:T(128)S(1)} %get-tuple-element.31, f32[3]{0:T(128)S(1)} %get-tuple-element.30, f32[3]{0:T(128)S(1)} %get-tuple-element.29, ...), kind=kLoop, calls=%fused_computation.55 | loop fusion | flops 737280 | bytes 1769568 | tf_op jit(solution)/shard_map/add | solution.py:42
  92.4 0.2 copy.22
  92.6 0.2 copy.30
  92.8 1.3 dynamic-slice
  94.1 31.2 %all-gather.2 = f32[16,1,3]{2,1,0:T(1,128)S(1)} all-gather(f32[1,1,3]{2,1,0:T(1,128)S(1)} %fusion.41), channel_id=1, replica_groups=mesh['grp'=2,'seq_0'=16,'seq_1'=8,'head'=2] {'seq_0'}, dimensions={0}, use_global_device_ids=true | all-gather | bytes 204 | tf_op jit(solution)/shard_map/all_gather | solution.py:25
  125.3 0.1 fusion.10
  125.5 0.1 fusion.9
  125.6 28.7 %all-reduce = f32[8,3,128]{2,0,1:T(8,128)S(1)} all-reduce(f32[8,3,128]{2,0,1:T(8,128)} %reduce-scatter.3.cloned.1.call-done), channel_id=4, replica_groups=mesh['grp'=2,'seq_0'=16,'seq_1'=8,'head'=2] {'seq_1'}, use_global_device_ids=true, to_apply=%region_3.4.clone | all-reduce | flops 3072 | bytes 24576
  154.3 1.2 constant_dynamic-slice_fusion
  155.5 42.0 %all-gather.6.cloned.1.call-done = f32[16,128,3,128]{3,1,2,0:T(8,128)} async-done(((f32[1,128,3,128]{3,1,2,0:T(8,128)}), f32[16,128,3,128]{3,1,2,0:T(8,128)}) %all-gather.6.cloned.1.call-update) | async-done | bytes 3145744 | tf_op jit(solution)/shard_map/all_gather | solution.py:25
  197.5 4.1 %fusion.3 = f32[384,3,128]{0,2,1:T(8,128)} fusion(bf16[384,3,128]{0,2,1:T(8,128)(2,1)S(1)} %bitcast.278, f32[384,3]{0,1:T(4,128)S(1)} %get-tuple-element.34, f32[16,128,3,128]{3,1,2,0:T(8,128)} %all-gather.6.cloned.1.call-done, f32[1024,3,128]{2,0,1:T(8,128)} %all-gather.8.cloned.1.call-done, f32[3]{0:T(128)S(1)} %get-tuple-element.25, ...), kind=kOutput, calls=%fused_computation.5 | convolution fusion | flops 41484288 | bytes 5608260 | tf_op jit(solution)/shard_map/thi,ihj->thj/dot_general | solution.py:86
  201.6 2.1 fusion.45
  203.7 0.1 multiply_reduce_fusion
  203.8 0.3 multiply_convert_fusion.1
  204.1 0.9 copy.31
  (19 shorter events, 0.3 us)
Async XLA Ops:
  8.0 81.9 %all-gather.8.cloned.1.call-start = ((), (), s32[]{:S(2)}) async-start(), calls=%async_computation.3 | async-start | bytes 1769472 | tf_op jit(solution)/shard_map/all_gather | solution.py:25
  10.5 81.9 %copy-start.1 = (bf16[384,384]{1,0:T(8,128)(2,1)S(1)}, bf16[384,384]{1,0:T(8,128)(2,1)}, u32[]{:S(2)}) copy-start(bf16[384,384]{1,0:T(8,128)(2,1)} %param.5) | copy-start | bytes 884740
  11.6 81.0 %copy-start = (bf16[384,384]{1,0:T(8,128)(2,1)S(1)}, bf16[384,384]{1,0:T(8,128)(2,1)}, u32[]{:S(2)}) copy-start(bf16[384,384]{1,0:T(8,128)(2,1)} %param.8) | copy-start | bytes 884740
  11.7 113.9 %reduce-scatter.3.cloned.1.call-start = ((), (), s32[]{:S(2)}) async-start(), calls=%async_computation.2 | async-start | bytes 208896 | tf_op jit(solution)/shard_map/reduce_scatter | solution.py:37
  12.3 185.2 %all-gather.6.cloned.1.call-start = ((), (), s32[]{:S(2)}) async-start(), calls=%async_computation.1 | async-start | bytes 3342336 | tf_op jit(solution)/shard_map/all_gather | solution.py:25
  201.6 2.2 %copy-start.2 = (f32[384]{0:T(512)S(1)}, f32[384]{0:T(512)}, u32[]{:S(2)}) copy-start(f32[384]{0:T(512)} %param.9) | copy-start | bytes 4612
Sparse Core Ops, SparseCore 0:
  11.8 78.0 all-gather.7
Sparse Core Ops, SparseCore 1:
  15.6 105.7 reduce-scatter.2
  123.2 74.2 all-gather.5
where the time goes:
time: 213 us; the launch traced here: 212 us
  blocking collectives  111 us (52%)
  waiting for transfers between devices  69.2 us (32%)
  between operations  15.7 us (7%)
  matrix products  7.21 us (3%)
  local copies, waits for them, and re-layouts  6.17 us (3%)
  other arithmetic  3.12 us (1%)
    all_gather x2, blocking collectives, carried_in(): pieces = jax.tree.map(lambda part: lax.all_gather(part, axis), so_far)  82.2 us
    all_gather x2, waiting for transfers between devices, carried_in(): pieces = jax.tree.map(lambda part: lax.all_gather(part, axis), so_far)  68.5 us
    unnamed x1, blocking collectives  28.7 us
    unnamed x12, local copies, waits for them, and re-layouts  5.98 us
  transfers between devices with their start and end apart: 3, of which 2 were waited for; matrix products, arithmetic and copies ran while one was open for 3% of the time, Pallas kernels for 0%

commit v1 on v0

v1 whole, which is shorter than its diff:
```python
import functools
import math

import jax
import jax.numpy as jnp
import numpy as np
from jax import lax
from jax.experimental import pallas as pl
from jax.experimental.pallas import tpu as pltpu
from jax.sharding import PartitionSpec as P

ALL_HEADS = 10
HEADS = 6
DH = 128
NX = 8
MESH = pl.DeviceIdType.MESH
F32 = jnp.float32
BF16 = jnp.bfloat16
SUB = 128


def log_decays(shards):
    per = HEADS // shards
    ids = ALL_HEADS - HEADS + np.arange(HEADS, dtype=np.float64)
    table = np.log1p(-np.exp2(-5.0 - ids)).reshape(shards, per)
    return [[float(np.float32(v)) for v in row] for row in table]


def kernel(
    table, nz,
    q_hbm, k_hbm, v_hbm, g_hbm, gain_ref,
    out_hbm, fin_ref,
    q_v, k_v, v_v, g_v, out_v,
    st, sx, rx, xp, rtot, rz, win, rw, cb, rc, carr, inner, gs, fs, fr,
    load_sem, store_sem, xs_sem, xr_sem, as_sem, ar_sem, ws_sem, wr_sem, bs_sem, br_sem, fs_sem, fr_sem, relay,
):
    tokens = q_v.shape[0]
    nh = q_v.shape[1] // DH
    rows = DH // NX
    nb = tokens // SUB
    scale = DH ** (-0.5)
    me = lax.axis_index("seq")
    z = lax.div(me, NX)
    x = lax.rem(me, NX)
    hd = lax.axis_index("head")

    lds = []
    for h in range(nh):
        ld = jnp.float32(table[0][h])
        for s in range(1, len(table)):
            ld = jnp.where(hd == s, jnp.float32(table[s][h]), ld)
        lds.append(ld)

    def at(zz, xx):
        return {"seq": zz * NX + xx}

    def zwrap(d):
        return lax.rem(z + (d % nz), nz)

    def xwrap(d):
        return lax.rem(x + (d % NX), NX)

    def load(src, dst, i, h):
        cols = pl.ds(h * DH, DH)
        return pltpu.make_async_copy(src.at[:, cols], dst.at[:, cols], load_sem.at[i, h])

    for h in range(nh):
        load(k_hbm, k_v, 0, h).start()
        load(v_hbm, v_v, 1, h).start()
    for h in range(nh):
        load(q_hbm, q_v, 2, h).start()
        load(g_hbm, g_v, 3, h).start()

    barrier = pltpu.get_barrier_semaphore()
    for d in range(1, NX):
        pl.semaphore_signal(barrier, inc=1, device_id=at(z, xwrap(d)), device_id_type=MESH)
    near = (1, -1, 2, -2, 3, -3)
    for d in near:
        pl.semaphore_signal(barrier, inc=1, device_id=at(zwrap(d), x), device_id_type=MESH)

    zero = jnp.zeros((nh, rows, DH), F32)

    @pl.when(z < 2)
    def _():
        rz[:, 0] = zero

    @pl.when(z < 1)
    def _():
        rz[:, 1] = zero

    @pl.when(z != 3)
    def _():
        rz[:, 3] = zero

    for j in range(4):
        @pl.when(z < 2 + 4 * j)
        def _(j=j):
            rw[:, j] = zero

    def r_iota(n):
        return lax.broadcasted_iota(jnp.int32, (n, DH), 0).astype(F32)

    def x_copy(h, d):
        to = xwrap(d)
        return pltpu.make_async_remote_copy(
            sx.at[h, to], rx.at[h, x], xs_sem.at[h, d], xr_sem.at[h, d],
            device_id=at(z, to), device_id_type=MESH)

    def x_wait(h, d):
        src = xwrap(-d)
        return pltpu.make_async_remote_copy(
            sx.at[h, src], rx.at[h, src], xs_sem.at[h, d], xr_sem.at[h, d],
            device_id=at(z, src), device_id_type=MESH)

    def b_copy(h, d):
        to = xwrap(d)
        return pltpu.make_async_remote_copy(
            cb.at[h, to], rc.at[h, x], bs_sem.at[h, d], br_sem.at[h, d],
            device_id=at(z, to), device_id_type=MESH)

    def b_wait(h, d):
        src = xwrap(-d)
        return pltpu.make_async_remote_copy(
            cb.at[h, src], rc.at[h, src], bs_sem.at[h, d], br_sem.at[h, d],
            device_id=at(z, src), device_id_type=MESH)

    last_c = nz - 3
    raw = (
        (0, 2, z <= last_c - 2),
        (3, 3, z == 0),
        (1, 1, z <= last_c - 1),
        (2, -1, (z >= 1) & (z <= last_c + 1)),
    )
    raw_in = ((0, (z >= 2) & (z <= last_c)), (3, z == 3), (1, (z >= 1) & (z <= last_c)), (2, z <= last_c))

    def a_copy(h, slot, d):
        return pltpu.make_async_remote_copy(
            rtot.at[h], rz.at[h, slot], as_sem.at[h, slot], ar_sem.at[h, slot],
            device_id=at(zwrap(d), x), device_id_type=MESH)

    def w_copy(h, j):
        return pltpu.make_async_remote_copy(
            win.at[h], rw.at[h, j], ws_sem.at[h, j], wr_sem.at[h, j],
            device_id=at(zwrap(2 + 4 * j), x), device_id_type=MESH)

    def f_copy(zz):
        return pltpu.make_async_remote_copy(
            fs.at[zz], fr, fs_sem.at[zz], fr_sem,
            device_id=at(zz, x), device_id_type=MESH)

    far = (4, 3, 5, 2, 6, 1, 7)

    for h in range(nh):
        cols = pl.ds(h * DH, DH)
        tail = jnp.exp((tokens - 1 - r_iota(tokens)) * lds[h])
        load(k_hbm, k_v, 0, h).wait()
        load(v_hbm, v_v, 1, h).wait()
        kd = (k_v[:, cols].astype(F32) * scale * tail).astype(BF16)
        st[h] = lax.dot_general(kd, v_v[:, cols], (((0,), (0,)), ((), ())), preferred_element_type=F32)
        for xx in range(NX):
            sx[h, xx] = st[h, pl.ds(xx, rows, stride=NX), :]
        if h == 0:
            pl.semaphore_wait(barrier, NX - 1 + len(near))
        for d in far:
            x_copy(h, d).start()
        rx[h, x] = sx[h, x]
        if h == 0:
            for d in (3, -3):
                pl.semaphore_signal(relay, inc=1, device_id=at(zwrap(d), x), device_id_type=MESH)

    ri = lax.broadcasted_iota(jnp.int32, (SUB, SUB), 0)
    ci = lax.broadcasted_iota(jnp.int32, (SUB, SUB), 1)

    def inner_of(h):
        cols = pl.ds(h * DH, DH)
        load(q_hbm, q_v, 2, h).wait()
        base = jnp.exp((ri - ci).astype(F32) * lds[h]) * scale
        diag = jnp.where(ri >= ci, base, 0.0)
        for i in range(nb):
            qi = q_v[pl.ds(i * SUB, SUB), cols]
            parts = []
            for j in range(i + 1):
                s = lax.dot_general(qi, k_v[pl.ds(j * SUB, SUB), cols], (((1,), (1,)), ((), ())),
                                    preferred_element_type=F32)
                if j == i:
                    w = jnp.where(ri >= ci, s * diag, 0.0)
                else:
                    w = s * (base * jnp.exp(lds[h] * float((i - j) * SUB)))
                parts.append(w.astype(BF16))
            w = parts[0] if i == 0 else jnp.concatenate(parts, axis=1)
            inner[h, pl.ds(i * SUB, SUB), :] = jnp.dot(
                w, v_v[pl.ds(0, (i + 1) * SUB), cols], preferred_element_type=F32)

    def gate_of(h):
        cols = pl.ds(h * DH, DH)
        load(g_hbm, g_v, 3, h).wait()
        gain = gain_ref[:, cols]
        u = g_v[:, cols].astype(F32)
        gs[h] = u / (1.0 + jnp.exp(-u)) * gain

    inner_of(0)

    for h in range(nh):
        d1 = jnp.exp(lds[h] * float(tokens))
        for d in far:
            x_wait(h, d).wait_recv()
        acc = rx[h, 0]
        for xx in range(1, NX):
            xp[h, xx] = acc
            acc = acc * d1 + rx[h, xx]
        rtot[h] = acc
        for slot, d, ok in raw:
            @pl.when(ok)
            def _(slot=slot, d=d, h=h):
                a_copy(h, slot, d).start()

    inner_of(1)

    pl.semaphore_wait(relay, 2)

    @pl.when(z <= last_c)
    def _():
        for h in range(nh):
            dd = [jnp.exp(lds[h] * float(tokens * NX * k)) for k in range(5)]
            for slot, ok in raw_in:
                @pl.when(ok)
                def _(slot=slot, h=h):
                    a_copy(h, slot, 0).wait_recv()
            win[h] = (rz[h, 2] + dd[1] * rtot[h] + dd[2] * rz[h, 1]
                      + dd[3] * rz[h, 0] + dd[4] * rz[h, 3])
            for j in (1, 2, 3, 0):
                @pl.when(z + 2 + 4 * j < nz)
                def _(j=j, h=h):
                    w_copy(h, j).start()

    inner_of(2)
    for h in range(nh):
        gate_of(h)

    for h in range(nh):
        for j in range(4):
            @pl.when(z >= 2 + 4 * j)
            def _(j=j, h=h):
                w_copy(h, j).wait_recv()

        @pl.when(z == 1)
        def _(h=h):
            rw[h, 0] = rz[h, 1]
        ee = rw[h, 0]
        for j in range(1, 4):
            ee = ee + rw[h, j] * jnp.exp(lds[h] * float(tokens * NX * 4 * j))
        cb[h, 0] = ee
        for xx in range(1, NX):
            cb[h, xx] = xp[h, xx] + ee * jnp.exp(lds[h] * float(tokens * xx))
        for d in far:
            b_copy(h, d).start()
        rc[h, x] = cb[h, x]

        @pl.when(z == nz - 1)
        def _(h=h, ee=ee):
            fs[:, h, :] = ee * jnp.exp(lds[h] * float(tokens * NX)) + rtot[h]

    @pl.when(z == nz - 1)
    def _():
        for zz in range(nz - 1):
            f_copy(zz).start()
        fin_ref[0] = fs[nz - 1]

    for h in range(nh):
        cols = pl.ds(h * DH, DH)
        lead = jnp.exp((r_iota(SUB) + 1.0) * lds[h])
        for d in far:
            b_wait(h, d).wait_recv()
        for xx in range(NX):
            carr[h, pl.ds(xx, rows, stride=NX), :] = rc[h, xx]
        low = carr[h].astype(BF16)
        for i in range(nb):
            rs = pl.ds(i * SUB, SUB)
            o = jnp.dot(q_v[rs, cols], low, preferred_element_type=F32)
            mix = inner[h, rs, :] + o * (lead * jnp.exp(lds[h] * float(i * SUB)))
            mean = jnp.sum(mix, axis=1, keepdims=True) * (1.0 / DH)
            cen = mix - mean
            var = jnp.sum(cen * cen, axis=1, keepdims=True) * (1.0 / DH)
            out_v[rs, cols] = (cen * lax.rsqrt(var + 1e-05) * gs[h, rs, :]).astype(BF16)
        pltpu.make_async_copy(out_v.at[:, cols], out_hbm.at[:, cols], store_sem.at[h]).start()

    @pl.when(z < nz - 1)
    def _():
        f_copy(0).wait_recv()
        fin_ref[0] = fr[...]

    @pl.when(z == nz - 1)
    def _():
        for zz in range(nz - 1):
            f_copy(zz).wait_send()

    for h in range(nh):
        for d in far:
            x_copy(h, d).wait_send()
            b_copy(h, d).wait_send()
        for slot, d, ok in raw:
            @pl.when(ok)
            def _(slot=slot, d=d, h=h):
                a_copy(h, slot, d).wait_send()
        for j in range(4):
            @pl.when((z <= last_c) & (z + 2 + 4 * j < nz))
            def _(j=j, h=h):
                w_copy(h, j).wait_send()
        cols = pl.ds(h * DH, DH)
        pltpu.make_async_copy(out_v.at[:, cols], out_hbm.at[:, cols], store_sem.at[h]).wait()


def body(table, nz, queries, key_rows, value_rows, gate_input, norm_gain):
    tokens, width = queries.shape
    nh = width // DH
    rows = DH // NX
    anyspace = pl.BlockSpec(memory_space=pl.ANY)
    vmem = pl.BlockSpec(memory_space=pltpu.VMEM)
    dma = pltpu.SemaphoreType.DMA
    wide = pltpu.VMEM((tokens, width), BF16)
    eight = pltpu.VMEM((nh, NX, rows, DH), F32)
    four = pltpu.VMEM((nh, 4, rows, DH), F32)
    one = pltpu.VMEM((nh, rows, DH), F32)
    square = pltpu.VMEM((nh, DH, DH), F32)
    tall = pltpu.VMEM((nh, tokens, DH), F32)
    return pl.pallas_call(
        functools.partial(kernel, table, nz),
        out_shape=(
            jax.ShapeDtypeStruct((tokens, width), BF16),
            jax.ShapeDtypeStruct((1, nh, DH), F32),
        ),
        in_specs=[anyspace, anyspace, anyspace, anyspace, vmem],
        out_specs=(anyspace, vmem),
        scratch_shapes=[
            wide, wide, wide, wide, wide,
            square, eight, eight, eight, one, four, one, four, eight, eight, square, tall, tall,
            pltpu.VMEM((nz, nh, DH), F32), pltpu.VMEM((nh, DH), F32),
            dma((4, nh)), dma((nh,)), dma((nh, NX)), dma((nh, NX)), dma((nh, 4)), dma((nh, 4)),
            dma((nh, 4)), dma((nh, 4)), dma((nh, NX)), dma((nh, NX)), dma((nz,)), dma,
            pltpu.SemaphoreType.REGULAR,
        ],
        compiler_params=pltpu.CompilerParams(collective_id=0, has_side_effects=True),
        name="retention",
    )(queries, key_rows, value_rows, gate_input, norm_gain.reshape(1, width))


def solution(mesh):
    table = log_decays(mesh.shape["head"])
    rows = ("grp", "seq")
    placed = (P(rows, "head"),) * 4 + (P("head"),)
    return jax.shard_map(
        functools.partial(body, table, mesh.shape["seq"] // NX),
        mesh=mesh,
        in_specs=placed,
        out_specs=(P(rows, "head"), P(rows, "head", None)),
        check_vma=False,
    )
```

time: 213 us -> 72.3 us (0.34)
  the two profiles are of different devices: /device:TPU:68 before, /device:TPU:80 now
where the time goes in v1:
time: 72.3 us; the launch traced here: 72 us
  Pallas kernels  67.2 us (93%)
  local copies, waits for them, and re-layouts  4.18 us (6%)
    pallas_call x1, Pallas kernels, body(): pl.pallas_call(functools.partial(kernel, table, nz), out_shape=(jax.Shape...  67.2 us
    unnamed x3, local copies, waits for them, and re-layouts  2.37 us

profile of v1, /device:TPU:80, one launch (start us, length us, event | category | flops | bytes accessed | tf_op | source)
XLA Modules:
  0.0 72.0 jit_solution(14393775671068534167)
XLA Ops:
  0.6 1.2 %reshape.7.gain_ref = f32[1,384]{1,0:T(1,128)} reshape(f32[384]{0:T(512)} %param.9) | data formatting | bytes 3072 | tf_op jit(solution)/shard_map/reshape | solution.py:344
  1.9 67.2 %retention.1 = (bf16[384,384]{1,0:T(8,128)(2,1)}, f32[1,3,128]{2,1,0:T(4,128)}) custom-call(bf16[384,384]{1,0:T(8,128)(2,1)} %q_hbm.1, bf16[384,384]{1,0:T(8,128)(2,1)} %k_hbm.1, bf16[384,384]{1,0:T(8,128)(2,1)} %v_hbm.1, bf16[384,384]{1,0:T(8,128)(2,1)} %g_hbm.1, f32[1,384]{1,0:T(1,128)} %reshape.7.gain_ref), custom_call_target="tpu_custom_call" | custom-call | tf_op jit(solution)/shard_map/retention/pallas_call | solution.py:326
  69.1 0.0 copy-start
  69.1 0.7 copy-done
  69.7 0.6 copy.7
  70.3 1.7 %copy.9 = bf16[384,384]{1,0:T(8,128)(2,1)} copy(bf16[384,384]{1,0:T(8,128)(2,1)} %get-tuple-element.6) | data formatting | bytes 589824
Async XLA Ops:
  69.1 0.7 copy-start

commit v2 on v1

v2 whole, which is shorter than its diff:
```python
import functools
import math

import jax
import jax.numpy as jnp
import numpy as np
from jax import lax
from jax.experimental import pallas as pl
from jax.experimental.pallas import tpu as pltpu
from jax.sharding import PartitionSpec as P

ALL_HEADS = 10
HEADS = 6
DH = 128
NX = 8
MESH = pl.DeviceIdType.MESH
F32 = jnp.float32
BF16 = jnp.bfloat16
SUB = 128


def log_decays(shards):
    per = HEADS // shards
    ids = ALL_HEADS - HEADS + np.arange(HEADS, dtype=np.float64)
    table = np.log1p(-np.exp2(-5.0 - ids)).reshape(shards, per)
    return [[float(np.float32(v)) for v in row] for row in table]


def kernel(
    table, nz,
    q_hbm, k_hbm, v_hbm, g_hbm, gain_hbm,
    out_ref, fin_ref,
    q_v, k_v, v_v, g_v, gain_v,
    st, sx, rx, xp, rtot, rz, win, rw, cb, rc, carr, inner, gs, fs, fr,
    load_sem, gain_sem, xs_sem, xr_sem, as_sem, ar_sem, ws_sem, wr_sem, bs_sem, br_sem, fs_sem, fr_sem, ready,
):
    tokens = q_v.shape[0]
    nh = q_v.shape[1] // DH
    rows = DH // NX
    nb = tokens // SUB
    scale = DH ** (-0.5)
    me = lax.axis_index("seq")
    z = lax.div(me, NX)
    x = lax.rem(me, NX)
    hd = lax.axis_index("head")
    last_c = nz - 3

    lds = []
    for h in range(nh):
        ld = jnp.float32(table[0][h])
        for s in range(1, len(table)):
            ld = jnp.where(hd == s, jnp.float32(table[s][h]), ld)
        lds.append(ld)

    def at(zz, xx):
        return {"seq": zz * NX + xx}

    def xwrap(d):
        return lax.rem(x + (d % NX), NX)

    def load(src, dst, i, h):
        cols = pl.ds(h * DH, DH)
        return pltpu.make_async_copy(src.at[:, cols], dst.at[:, cols], load_sem.at[i, h])

    def gain_load():
        return pltpu.make_async_copy(gain_hbm, gain_v, gain_sem)

    for h in range(nh):
        load(k_hbm, k_v, 0, h).start()
        load(v_hbm, v_v, 1, h).start()

    barrier = pltpu.get_barrier_semaphore()
    for d in range(1, NX):
        pl.semaphore_signal(barrier, inc=1, device_id=at(z, xwrap(d)), device_id_type=MESH)
    for zz in range(1, nz):
        @pl.when(z < zz)
        def _(zz=zz):
            pl.semaphore_signal(barrier, inc=1, device_id=at(zz, x), device_id_type=MESH)

    for h in range(nh):
        load(q_hbm, q_v, 2, h).start()
        load(g_hbm, g_v, 3, h).start()
    gain_load().start()

    zero = jnp.zeros((nh, rows, DH), F32)

    @pl.when(z < 2)
    def _():
        rz[:, 0] = zero

    @pl.when(z < 1)
    def _():
        rz[:, 1] = zero

    @pl.when(z != 3)
    def _():
        rz[:, 3] = zero

    for j in range(4):
        @pl.when(z < 2 + 4 * j)
        def _(j=j):
            rw[:, j] = zero

    for zz in range(nz):
        @pl.when(zz <= z)
        def _(zz=zz):
            fr[zz] = jnp.zeros((nh, DH), F32)

    def r_iota(n):
        return lax.broadcasted_iota(jnp.int32, (n, DH), 0).astype(F32)

    def x_copy(h, d):
        to = xwrap(d)
        return pltpu.make_async_remote_copy(
            sx.at[h, to], rx.at[h, x], xs_sem.at[h, d], xr_sem.at[h, d],
            device_id=at(z, to), device_id_type=MESH)

    def x_wait(h, d):
        src = xwrap(-d)
        return pltpu.make_async_remote_copy(
            sx.at[h, src], rx.at[h, src], xs_sem.at[h, d], xr_sem.at[h, d],
            device_id=at(z, src), device_id_type=MESH)

    def b_copy(h, d):
        to = xwrap(d)
        return pltpu.make_async_remote_copy(
            cb.at[h, to], rc.at[h, x], bs_sem.at[h, d], br_sem.at[h, d],
            device_id=at(z, to), device_id_type=MESH)

    def b_wait(h, d):
        src = xwrap(-d)
        return pltpu.make_async_remote_copy(
            cb.at[h, src], rc.at[h, src], bs_sem.at[h, d], br_sem.at[h, d],
            device_id=at(z, src), device_id_type=MESH)

    raw = (
        (2, -1, (z >= 1) & (z <= last_c + 1)),
        (1, 1, z <= last_c - 1),
        (0, 2, z <= last_c - 2),
        (3, 3, z == 0),
    )
    raw_in = ((0, (z >= 2) & (z <= last_c)), (3, z == 3), (1, (z >= 1) & (z <= last_c)), (2, z <= last_c))

    def a_copy(h, slot, d):
        return pltpu.make_async_remote_copy(
            rtot.at[h], rz.at[h, slot], as_sem.at[h, slot], ar_sem.at[h, slot],
            device_id=at(z + d, x), device_id_type=MESH)

    def w_copy(h, j):
        return pltpu.make_async_remote_copy(
            win.at[h], rw.at[h, j], ws_sem.at[h, j], wr_sem.at[h, j],
            device_id=at(z + (2 + 4 * j), x), device_id_type=MESH)

    def f_copy(zz):
        return pltpu.make_async_remote_copy(
            fs.at[zz], fr.at[z], fs_sem.at[zz], fr_sem.at[z],
            device_id=at(zz, x), device_id_type=MESH)

    def f_wait(zz):
        return pltpu.make_async_remote_copy(
            fs.at[zz], fr.at[zz], fs_sem.at[zz], fr_sem.at[zz],
            device_id=at(zz, x), device_id_type=MESH)

    readies = ((1, (z >= 1) & (z <= last_c)), (2, z >= 2), (3, z == 3)) + tuple(
        (2 + 4 * j, z >= 2 + 4 * j) for j in range(1, 4))
    slot_of = {d: i for i, (d, _) in enumerate(readies)}

    def ready_wait(d):
        pl.semaphore_wait(ready.at[slot_of[d]], 1)

    far = (4, 3, 5, 2, 6, 1, 7)

    for h in range(nh):
        cols = pl.ds(h * DH, DH)
        tail = jnp.exp((tokens - 1 - r_iota(tokens)) * lds[h]) * scale
        with jax.named_scope(f"load{h}"):
            load(k_hbm, k_v, 0, h).wait()
            load(v_hbm, v_v, 1, h).wait()
        with jax.named_scope(f"state{h}"):
            kd = (k_v[:, cols].astype(F32) * tail).astype(BF16)
            st[h] = lax.dot_general(kd, v_v[:, cols], (((0,), (0,)), ((), ())), preferred_element_type=F32)
            for xx in range(NX):
                sx[h, xx] = st[h, pl.ds(xx, rows, stride=NX), :]
        if h == 0:
            with jax.named_scope("barrier"):
                pl.semaphore_wait(barrier, NX - 1 + z)
        for d in far:
            x_copy(h, d).start()
        rx[h, x] = sx[h, x]
    for d, ok in readies:
        @pl.when(ok)
        def _(d=d):
            pl.semaphore_signal(ready.at[slot_of[d]], inc=1, device_id=at(z - d, x), device_id_type=MESH)

    ri = lax.broadcasted_iota(jnp.int32, (SUB, SUB), 0)
    ci = lax.broadcasted_iota(jnp.int32, (SUB, SUB), 1)

    def inner_of(h):
        cols = pl.ds(h * DH, DH)
        load(q_hbm, q_v, 2, h).wait()
        base = jnp.exp((ri - ci).astype(F32) * lds[h]) * scale
        for i in range(nb):
            qi = q_v[pl.ds(i * SUB, SUB), cols]
            parts = []
            for j in range(i + 1):
                s = lax.dot_general(qi, k_v[pl.ds(j * SUB, SUB), cols], (((1,), (1,)), ((), ())),
                                    preferred_element_type=F32)
                if j == i:
                    w = jnp.where(ri >= ci, s * base, 0.0)
                else:
                    w = s * (base * jnp.exp(lds[h] * float((i - j) * SUB)))
                parts.append(w.astype(BF16))
            w = parts[0] if i == 0 else jnp.concatenate(parts, axis=1)
            inner[h, pl.ds(i * SUB, SUB), :] = jnp.dot(
                w, v_v[pl.ds(0, (i + 1) * SUB), cols], preferred_element_type=F32)

    def gate_of(h):
        cols = pl.ds(h * DH, DH)
        load(g_hbm, g_v, 3, h).wait()
        gain = gain_v[pl.ds(h * DH, DH)].reshape(1, DH)
        u = g_v[:, cols].astype(F32)
        gs[h] = u / (1.0 + jnp.exp(-u)) * gain

    def local_work():
        with jax.named_scope("local"):
            gain_load().wait()
            for h in range(nh):
                inner_of(h)
                gate_of(h)

    for h in range(nh):
        d1 = jnp.exp(lds[h] * float(tokens))
        with jax.named_scope(f"xwait{h}"):
            for d in far:
                x_wait(h, d).wait_recv()
        with jax.named_scope(f"prefix{h}"):
            acc = rx[h, 0]
            for xx in range(1, NX):
                xp[h, xx] = acc
                acc = acc * d1 + rx[h, xx]
            rtot[h] = acc
            fs[:, h, :] = acc * jnp.exp((nz - 1 - z).astype(F32) * (lds[h] * float(tokens * NX)))

    for zz in range(nz - 1):
        @pl.when(z > zz)
        def _(zz=zz):
            f_copy(zz).start()
    for slot, d, ok in raw:
        @pl.when(ok)
        def _(slot=slot, d=d):
            if d > 0:
                ready_wait(d)
            for h in range(nh):
                a_copy(h, slot, d).start()

    early = (z >= 1) & (z < nz // 2)

    @pl.when(early)
    def _():
        local_work()

    @pl.when(z <= last_c)
    def _():
        with jax.named_scope("windows"):
            @pl.when(z > last_c - 2)
            def _():
                ready_wait(2)
            for h in range(nh):
                dd = [jnp.exp(lds[h] * float(tokens * NX * k)) for k in range(5)]
                for slot, ok in raw_in:
                    @pl.when(ok)
                    def _(slot=slot, h=h):
                        pltpu.make_async_remote_copy(
                            rtot.at[h], rz.at[h, slot], as_sem.at[h, slot], ar_sem.at[h, slot],
                            device_id=at(z, x), device_id_type=MESH).wait_recv()
                win[h] = (rz[h, 2] + dd[1] * rtot[h] + dd[2] * rz[h, 1]
                          + dd[3] * rz[h, 0] + dd[4] * rz[h, 3])
                w_copy(h, 0).start()

    for h in range(nh):
        with jax.named_scope(f"wwait{h}"):
            for j in range(4):
                @pl.when(z >= 2 + 4 * j)
                def _(j=j, h=h):
                    pltpu.make_async_remote_copy(
                        win.at[h], rw.at[h, j], ws_sem.at[h, j], wr_sem.at[h, j],
                        device_id=at(z, x), device_id_type=MESH).wait_recv()

            @pl.when(z == 1)
            def _(h=h):
                rw[h, 0] = rz[h, 1]
        ee = rw[h, 0]
        for j in range(1, 4):
            ee = ee + rw[h, j] * jnp.exp(lds[h] * float(tokens * NX * 4 * j))
        cb[h, 0] = ee
        for xx in range(1, NX):
            cb[h, xx] = xp[h, xx] + ee * jnp.exp(lds[h] * float(tokens * xx))
        for d in far:
            b_copy(h, d).start()
        rc[h, x] = cb[h, x]

    @pl.when(jnp.logical_not(early))
    def _():
        local_work()

    for h in range(nh):
        cols = pl.ds(h * DH, DH)
        lead = jnp.exp((r_iota(SUB) + 1.0) * lds[h])
        with jax.named_scope(f"bwait{h}"):
            for d in far:
                b_wait(h, d).wait_recv()
        with jax.named_scope(f"outer{h}"):
            for xx in range(NX):
                carr[h, pl.ds(xx, rows, stride=NX), :] = rc[h, xx]
            low = carr[h].astype(BF16)
            for i in range(nb):
                rs = pl.ds(i * SUB, SUB)
                o = jnp.dot(q_v[rs, cols], low, preferred_element_type=F32)
                mix = inner[h, rs, :] + o * (lead * jnp.exp(lds[h] * float(i * SUB)))
                mean = jnp.sum(mix, axis=1, keepdims=True) * (1.0 / DH)
                cen = mix - mean
                var = jnp.sum(cen * cen, axis=1, keepdims=True) * (1.0 / DH)
                out_ref[rs, cols] = (cen * lax.rsqrt(var + 1e-05) * gs[h, rs, :]).astype(BF16)

    for j in range(1, 4):
        @pl.when(z + 2 + 4 * j < nz)
        def _(j=j):
            ready_wait(2 + 4 * j)
            for h in range(nh):
                w_copy(h, j).start()

    ahead = (nz - 1 - z).astype(F32)
    mine = []
    for h in range(nh):
        one = lds[h] * float(tokens * NX)
        mine.append(jnp.exp((ahead + 1.0) * one) * cb[h, 0, pl.ds(z, 1), :]
                    + jnp.exp(ahead * one) * rtot[h, pl.ds(z, 1), :])
    with jax.named_scope("fwait"):
        for zz in range(1, nz):
            @pl.when(z < zz)
            def _(zz=zz):
                f_wait(zz).wait_recv()
    for h in range(nh):
        fin_ref[h] = mine[h] + jnp.sum(fr[:, h, :], axis=0, keepdims=True)

    with jax.named_scope("ends"):
        for zz in range(nz - 1):
            @pl.when(z > zz)
            def _(zz=zz):
                f_copy(zz).wait_send()
        for h in range(nh):
            for d in far:
                x_copy(h, d).wait_send()
                b_copy(h, d).wait_send()
        for slot, d, ok in raw:
            @pl.when(ok)
            def _(slot=slot, d=d):
                for h in range(nh):
                    a_copy(h, slot, d).wait_send()
        for j in range(4):
            @pl.when(z + 2 + 4 * j < nz)
            def _(j=j):
                for h in range(nh):
                    w_copy(h, j).wait_send()


def body(table, nz, queries, key_rows, value_rows, gate_input, norm_gain):
    tokens, width = queries.shape
    nh = width // DH
    rows = DH // NX
    anyspace = pl.BlockSpec(memory_space=pl.ANY)
    vmem = pl.BlockSpec(memory_space=pltpu.VMEM)
    dma = pltpu.SemaphoreType.DMA
    wide = pltpu.VMEM((tokens, width), BF16)
    eight = pltpu.VMEM((nh, NX, rows, DH), F32)
    four = pltpu.VMEM((nh, 4, rows, DH), F32)
    one = pltpu.VMEM((nh, rows, DH), F32)
    square = pltpu.VMEM((nh, DH, DH), F32)
    tall = pltpu.VMEM((nh, tokens, DH), F32)
    retained, final = pl.pallas_call(
        functools.partial(kernel, table, nz),
        out_shape=(pltpu.VMEM((tokens, width), BF16), pltpu.VMEM((nh, 1, DH), F32)),
        in_specs=[anyspace] * 5,
        out_specs=(vmem, vmem),
        scratch_shapes=[
            wide, wide, wide, wide, pltpu.VMEM((width,), F32),
            square, eight, eight, eight, one, four, one, four, eight, eight, square, tall, tall,
            pltpu.VMEM((nz, nh, DH), F32), pltpu.VMEM((nz, nh, DH), F32),
            dma((4, nh)), dma, dma((nh, NX)), dma((nh, NX)), dma((nh, 4)), dma((nh, 4)),
            dma((nh, 4)), dma((nh, 4)), dma((nh, NX)), dma((nh, NX)), dma((nz,)), dma((nz,)),
            pltpu.SemaphoreType.REGULAR((6,)),
        ],
        compiler_params=pltpu.CompilerParams(collective_id=0, has_side_effects=True),
        name="retention",
    )(queries, key_rows, value_rows, gate_input, norm_gain)
    return retained, final.reshape(1, nh, DH)


def solution(mesh):
    table = log_decays(mesh.shape["head"])
    rows = ("grp", "seq")
    placed = (P(rows, "head"),) * 4 + (P("head"),)
    return jax.shard_map(
        functools.partial(body, table, mesh.shape["seq"] // NX),
        mesh=mesh,
        in_specs=placed,
        out_specs=(P(rows, "head"), P(rows, "head", None)),
        check_vma=False,
    )
```

time: 72.3 us -> 61.7 us (0.85)
  the two profiles are of different devices: /device:TPU:80 before, /device:TPU:66 now
where the time goes in v2:
time: 61.7 us; the launch traced here: 61.6 us
  Pallas kernels  59.6 us (97%)
  local copies, waits for them, and re-layouts  1.28 us (2%)
  between operations  0.64 us (1%)
    pallas_call x1, Pallas kernels, body(): pl.pallas_call(functools.partial(kernel, table, nz), out_shape=(pltpu.VME...  59.6 us
    unnamed x2, local copies, waits for them, and re-layouts  1.28 us

profile of v2, /device:TPU:66, one launch (start us, length us, event | category | flops | bytes accessed | tf_op | source)
XLA Modules:
  0.0 61.6 jit_solution(14282474422942291853)
XLA Ops:
  0.6 59.6 %retention.1 = (bf16[384,384]{1,0:T(8,128)(2,1)S(1)}, f32[3,1,128]{2,1,0:T(1,128)S(1)}) custom-call(bf16[384,384]{1,0:T(8,128)(2,1)} %q_hbm.1, bf16[384,384]{1,0:T(8,128)(2,1)} %k_hbm.1, bf16[384,384]{1,0:T(8,128)(2,1)} %v_hbm.1, bf16[384,384]{1,0:T(8,128)(2,1)} %g_hbm.1, f32[384]{0:T(512)} %gain_hbm.1), custom_call_target="tpu_custom_call" | custom-call | tf_op jit(solution)/shard_map/retention/pallas_call | solution.py:380
  60.3 0.7 %copy.9 = bf16[384,384]{1,0:T(8,128)(2,1)} copy(bf16[384,384]{1,0:T(8,128)(2,1)S(1)} %get-tuple-element.6) | data formatting | bytes 589824
  61.0 0.6 copy.10

commit v3 on v2

v3 whole, which is shorter than its diff:
```python
import functools
import math

import jax
import jax.numpy as jnp
import numpy as np
from jax import lax
from jax.experimental import pallas as pl
from jax.experimental.pallas import tpu as pltpu
from jax.sharding import PartitionSpec as P

ALL_HEADS = 10
HEADS = 6
DH = 128
NX = 8
MESH = pl.DeviceIdType.MESH
F32 = jnp.float32
BF16 = jnp.bfloat16
SUB = 128


def log_decays(shards):
    per = HEADS // shards
    ids = ALL_HEADS - HEADS + np.arange(HEADS, dtype=np.float64)
    table = np.log1p(-np.exp2(-5.0 - ids)).reshape(shards, per)
    return [[float(np.float32(v)) for v in row] for row in table]


def kernel(
    table, nz,
    q_hbm, k_hbm, v_hbm, g_hbm, gain_hbm,
    out_ref, fin_ref,
    q_v, k_v, v_v, g_v, gain_v,
    st, sx, rx, xp, rtot, rz, win, rw, cb, rc, carr, inner, gs, fs, fr, es, er,
    kv_sem, in_sem, xs_sem, xr_sem, as_sem, ar_sem, ws_sem, wr_sem, bs_sem, br_sem, fs_sem, fr_sem, es_sem, er_sem, ready, xready,
):
    tokens = q_v.shape[0]
    nh = q_v.shape[1] // DH
    rows = DH // NX
    nb = tokens // SUB
    scale = DH ** (-0.5)
    me = lax.axis_index("seq")
    z = lax.div(me, NX)
    x = lax.rem(me, NX)
    hd = lax.axis_index("head")
    plane = (lax.axis_index("grp") == 0) & (hd == 0)
    column = plane & (x == 0)
    first = column & (z == 0)
    inner_col = column & (z > 0) & (z < nz - 1)
    last_c = nz - 3

    lds = []
    for h in range(nh):
        ld = jnp.float32(table[0][h])
        for s in range(1, len(table)):
            ld = jnp.where(hd == s, jnp.float32(table[s][h]), ld)
        lds.append(ld)

    def at(zz, xx):
        return {"seq": zz * NX + xx}

    def xwrap(d):
        return lax.rem(x + (d % NX), NX)

    def load(src, dst, h):
        cols = pl.ds(h * DH, DH)
        return pltpu.make_async_copy(src.at[:, cols], dst.at[:, cols], kv_sem.at[h])

    def kv_wait(h):
        two = pl.ds(0, 2 * DH)
        pltpu.make_async_copy(k_hbm.at[:, two], k_v.at[:, two], kv_sem.at[h]).wait()

    whole = (
        pltpu.make_async_copy(q_hbm, q_v, in_sem.at[0]),
        pltpu.make_async_copy(g_hbm, g_v, in_sem.at[1]),
        pltpu.make_async_copy(gain_hbm, gain_v, in_sem.at[2]),
    )

    for h in range(nh):
        load(k_hbm, k_v, h).start()
        load(v_hbm, v_v, h).start()

    def key_of(xx):
        k = jnp.where(xx < NX // 2, xx, 3 * NX // 2 - 1 - xx)
        return jnp.where((xx == 0) & (z == 0) & plane, NX, k)

    def x_of(k):
        if k == NX:
            return 0
        return k if k < NX // 2 else 3 * NX // 2 - 1 - k

    key = key_of(x)

    barrier = pltpu.get_barrier_semaphore()
    for d in range(1, NX):
        @pl.when(key_of(xwrap(d)) > key)
        def _(d=d):
            pl.semaphore_signal(barrier, inc=1, device_id=at(z, xwrap(d)), device_id_type=MESH)
    last = z == nz - 1
    express = ((0, 0), (1, 0), (0, 1))

    def tell_later():
        for zz in range(1, nz):
            ok = z < zz
            if zz < nz - 1:
                ok = ok & jnp.logical_not(first)

            @pl.when(ok)
            def _(zz=zz):
                pl.semaphore_signal(barrier, inc=1, device_id=at(zz, x), device_id_type=MESH)

    @pl.when(z > 0)
    def _():
        tell_later()

    @pl.when(inner_col)
    def _():
        pl.semaphore_signal(barrier, inc=1, device_id=at(0, x), device_id_type=MESH)
    owed = jnp.where(plane, NX - 1 - jnp.where(x == 0, 0, 1), NX - 1)
    count = key + z + jnp.where(last, owed + NX - 1, jnp.where(z == nz - 2, owed, 0))
    count = jnp.where((z == 0) & plane, key - 1, count)
    count = jnp.where(first, NX + nz - 3, count) - jnp.where(inner_col, 1, 0)
    with jax.named_scope("barrier"):
        @pl.when(count > 0)
        def _():
            pl.semaphore_wait(barrier, count)
    for d in range(1, NX):
        @pl.when(key_of(xwrap(d)) < key)
        def _(d=d):
            pl.semaphore_signal(xready.at[NX - d], inc=1, device_id=at(z, xwrap(d)), device_id_type=MESH)

    @pl.when(z == 0)
    def _():
        tell_later()

    @pl.when(first)
    def _():
        for zz in range(1, nz - 1):
            pl.semaphore_signal(xready.at[0], inc=1, device_id=at(zz, x), device_id_type=MESH)
    for j, k in express:
        @pl.when((z == j) & jnp.logical_not(first))
        def _(k=k):
            for d in range(1, NX):
                pl.semaphore_signal(barrier, inc=1, device_id=at(nz - 1 - k, xwrap(d)), device_id_type=MESH)
    for c in whole:
        c.start()

    def r_iota(n):
        return lax.broadcasted_iota(jnp.int32, (n, DH), 0).astype(F32)

    def x_copy(h, to):
        return pltpu.make_async_remote_copy(
            sx.at[to, h], rx.at[x, h], xs_sem, xr_sem,
            device_id=at(z, to), device_id_type=MESH)

    def x_copy_all(to):
        return pltpu.make_async_remote_copy(
            sx.at[to], rx.at[x], xs_sem, xr_sem,
            device_id=at(z, to), device_id_type=MESH)

    def b_copy(h, d):
        to = xwrap(d)
        return pltpu.make_async_remote_copy(
            cb.at[h, to], rc.at[h, x], bs_sem, br_sem.at[h],
            device_id=at(z, to), device_id_type=MESH)

    def e_copy(j, k, to):
        return pltpu.make_async_remote_copy(
            es.at[j, to], er.at[k, x], es_sem, er_sem,
            device_id=at(j, to), device_id_type=MESH)

    def moved(ref, sem):
        return pltpu.make_async_copy(ref, ref, sem)

    def moved_some(ref, sem, n):
        for m in range(1, ref.shape[0]):
            @pl.when(n == m)
            def _(m=m):
                moved(ref.at[pl.ds(0, m)], sem).wait()

    raw = (
        (1, 1, z <= last_c - 1),
        (0, 2, z <= last_c - 2),
        (3, 3, z == 0),
        (2, -1, (z >= 1) & (z <= last_c + 1)),
    )
    raw_in = ((0, (z >= 2) & (z <= last_c)), (3, z == 3), (1, (z >= 1) & (z <= last_c)), (2, z <= last_c))

    def a_copy(slot, d):
        return pltpu.make_async_remote_copy(
            rtot, rz.at[slot], as_sem.at[slot], ar_sem.at[slot],
            device_id=at(z + d, x), device_id_type=MESH)

    def w_copy(j):
        return pltpu.make_async_remote_copy(
            win, rw.at[j], ws_sem.at[j], wr_sem.at[j],
            device_id=at(z + (2 + 4 * j), x), device_id_type=MESH)

    def f_copy(zz):
        return pltpu.make_async_remote_copy(
            fs.at[zz], fr.at[z], fs_sem, fr_sem,
            device_id=at(zz, x), device_id_type=MESH)

    readies = ((1, (z >= 1) & (z <= last_c)), (2, z >= 2), (3, z == 3)) + tuple(
        (2 + 4 * j, z >= 2 + 4 * j) for j in range(1, 4))
    slot_of = {d: i for i, (d, _) in enumerate(readies)}

    def ready_wait(d):
        @pl.when(jnp.logical_not(first))
        def _():
            pl.semaphore_wait(ready.at[slot_of[d]], 1)

    far = (4, 3, 5, 2, 6, 1, 7)

    for h in range(nh):
        cols = pl.ds(h * DH, DH)
        tail = jnp.exp((tokens - 1 - r_iota(tokens)) * lds[h]) * scale
        with jax.named_scope(f"load{h}"):
            kv_wait(h)
        with jax.named_scope(f"state{h}"):
            kd = (k_v[:, cols].astype(F32) * tail).astype(BF16)
            st[h] = lax.dot_general(kd, v_v[:, cols], (((0,), (0,)), ((), ())), preferred_element_type=F32)
            for xx in range(NX):
                sx[xx, h] = st[h, pl.ds(xx, rows, stride=NX), :]
        for d in far:
            @pl.when((key_of(xwrap(d)) < key) & (z < nz - 2))
            def _(d=d, h=h):
                x_copy(h, xwrap(d)).start()

    for r in range(nh, es.shape[2]):
        es[:, :, r, :] = jnp.zeros((2, NX, DH), F32)

    @pl.when(z >= nz - 2)
    def _():
        for h in range(nh):
            w = (NX - 1 - x + NX * (nz - 1 - z)).astype(F32) * (lds[h] * float(tokens))
            for j in range(2):
                es[j, :, h, :] = st[h, pl.ds(j * NX, NX), :] * jnp.exp(w)
        for j, k in express:
            for d in far + (0,):
                to = xwrap(d)
                ok = z == nz - 1 - k
                if j == 0:
                    ok = ok & jnp.logical_not(plane & (to == 0))

                @pl.when(ok)
                def _(j=j, k=k, to=to):
                    e_copy(j, k, to).start()
        for d in far:
            @pl.when(key_of(xwrap(d)) < key)
            def _(d=d):
                x_copy_all(xwrap(d)).start()
    for d, ok in readies:
        @pl.when(ok & jnp.logical_not(column & (z == d)))
        def _(d=d):
            pl.semaphore_signal(ready.at[slot_of[d]], inc=1, device_id=at(z - d, x), device_id_type=MESH)

    zero = jnp.zeros((nh, rows, DH), F32)

    @pl.when(z < 2)
    def _():
        rz[0] = zero

    @pl.when(z < 1)
    def _():
        rz[1] = zero

    @pl.when(z != 3)
    def _():
        rz[3] = zero

    for j in range(1, 4):
        @pl.when((z > 0) & (z < 2 + 4 * j))
        def _(j=j):
            rw[j] = zero

    for zz in range(nz):
        ok = zz <= z
        for j, k in express:
            if zz == nz - 1 - k:
                ok = ok | ((z == j) & jnp.logical_not(first))

        @pl.when(ok)
        def _(zz=zz):
            fr[zz] = jnp.zeros(fr.shape[1:], F32)
    for r in range(nh, fs.shape[1]):
        fs[:, r, :] = jnp.zeros((nz, DH), F32)
    rx[x] = sx[x]
    with jax.named_scope("xready"):
        for k in range(1, NX + 1):
            to = x_of(k)

            @pl.when((key < k) & (z == 0) & plane if k == NX else key < k)
            def _(to=to):
                pl.semaphore_wait(xready.at[lax.rem(to + NX - x, NX)], 1)
                x_copy_all(to).start()

    ri = lax.broadcasted_iota(jnp.int32, (SUB, SUB), 0)
    ci = lax.broadcasted_iota(jnp.int32, (SUB, SUB), 1)

    def inner_of(h):
        cols = pl.ds(h * DH, DH)
        base = jnp.exp((ri - ci).astype(F32) * lds[h]) * scale
        for i in range(nb):
            qi = q_v[pl.ds(i * SUB, SUB), cols]
            parts = []
            for j in range(i + 1):
                s = lax.dot_general(qi, k_v[pl.ds(j * SUB, SUB), cols], (((1,), (1,)), ((), ())),
                                    preferred_element_type=F32)
                if j == i:
                    w = jnp.where(ri >= ci, s * base, 0.0)
                else:
                    w = s * (base * jnp.exp(lds[h] * float((i - j) * SUB)))
                parts.append(w.astype(BF16))
            w = parts[0] if i == 0 else jnp.concatenate(parts, axis=1)
            inner[h, pl.ds(i * SUB, SUB), :] = jnp.dot(
                w, v_v[pl.ds(0, (i + 1) * SUB), cols], preferred_element_type=F32)

    def gate_of(h):
        cols = pl.ds(h * DH, DH)
        gain = gain_v[pl.ds(h * DH, DH)].reshape(1, DH)
        u = g_v[:, cols].astype(F32)
        gs[h] = u / (1.0 + jnp.exp(-u)) * gain

    def local_work():
        with jax.named_scope("local"):
            for c in whole:
                c.wait()
            for h in range(nh):
                inner_of(h)
                gate_of(h)

    with jax.named_scope("xwait"):
        moved(rx.at[pl.ds(0, NX - 1)], xr_sem).wait()
    with jax.named_scope("prefix"):
        for h in range(nh):
            d1 = jnp.exp(lds[h] * float(tokens))
            acc = rx[0, h]
            for xx in range(1, NX):
                xp[h, xx] = acc
                acc = acc * d1 + rx[xx, h]
            rtot[h] = acc
            fs[:, h, :] = acc * jnp.exp((nz - 1 - z).astype(F32) * (lds[h] * float(tokens * NX)))

    for zz in range(nz - 1):
        ok = z > zz
        for j, k in express:
            if zz == j:
                ok = ok & ((z != nz - 1 - k) | column if j == 0 else z != nz - 1 - k)
        if zz == 0:
            ok = ok & jnp.logical_not(inner_col)

        @pl.when(ok)
        def _(zz=zz):
            f_copy(zz).start()
    for slot, d, ok in raw:
        @pl.when(ok)
        def _(slot=slot, d=d):
            if d > 0:
                ready_wait(d)
            else:
                @pl.when(column & (z == 1))
                def _():
                    pl.semaphore_wait(xready.at[0], 1)
            a_copy(slot, d).start()

    def back(h):
        for d in far:
            b_copy(h, d).start()
        rc[h, x] = cb[h, x]

    @pl.when(z == 0)
    def _():
        for h in range(nh):
            cb[h, 0] = jnp.zeros((rows, DH), F32)
            for xx in range(1, NX):
                cb[h, xx] = xp[h, xx]
            back(h)

    early = (z >= 1) & (z < nz // 2)

    @pl.when(early)
    def _():
        local_work()

    @pl.when(z <= last_c)
    def _():
        with jax.named_scope("windows"):
            @pl.when(z > last_c - 2)
            def _():
                ready_wait(2)
            for slot, ok in raw_in:
                @pl.when(ok)
                def _(slot=slot):
                    moved(rz.at[slot], ar_sem.at[slot]).wait()
            for h in range(nh):
                dd = [jnp.exp(lds[h] * float(tokens * NX * k)) for k in range(5)]
                win[h] = (rz[2, h] + dd[1] * rtot[h] + dd[2] * rz[1, h]
                          + dd[3] * rz[0, h] + dd[4] * rz[3, h])
            w_copy(0).start()

    with jax.named_scope("wwait"):
        for j in range(4):
            @pl.when(z >= 2 + 4 * j)
            def _(j=j):
                moved(rw.at[j], wr_sem.at[j]).wait()

    @pl.when(z == 1)
    def _():
        rw[0] = rz[1]
    @pl.when(z > 0)
    def _():
        for h in range(nh):
            ee = rw[0, h]
            for j in range(1, 4):
                ee = ee + rw[j, h] * jnp.exp(lds[h] * float(tokens * NX * 4 * j))
            cb[h, 0] = ee
            for xx in range(1, NX):
                cb[h, xx] = xp[h, xx] + ee * jnp.exp(lds[h] * float(tokens * xx))
            back(h)

    @pl.when(inner_col)
    def _():
        @pl.when(z > 1)
        def _():
            pl.semaphore_wait(xready.at[0], 1)
        f_copy(0).start()

    for j in range(1, 4):
        @pl.when(z + 2 + 4 * j < nz)
        def _(j=j):
            ready_wait(2 + 4 * j)
            w_copy(j).start()

    @pl.when(jnp.logical_not(early))
    def _():
        local_work()

    for h in range(nh):
        cols = pl.ds(h * DH, DH)
        lead = jnp.exp((r_iota(SUB) + 1.0) * lds[h])
        with jax.named_scope(f"bwait{h}"):
            moved(rc.at[h, pl.ds(0, NX - 1)], br_sem.at[h]).wait()
        with jax.named_scope(f"outer{h}"):
            for xx in range(NX):
                carr[h, pl.ds(xx, rows, stride=NX), :] = rc[h, xx]
            low = carr[h].astype(BF16)
            for i in range(nb):
                rs = pl.ds(i * SUB, SUB)
                o = jnp.dot(q_v[rs, cols], low, preferred_element_type=F32)
                mix = inner[h, rs, :] + o * (lead * jnp.exp(lds[h] * float(i * SUB)))
                mean = jnp.sum(mix, axis=1, keepdims=True) * (1.0 / DH)
                cen = mix - mean
                var = jnp.sum(cen * cen, axis=1, keepdims=True) * (1.0 / DH)
                out_ref[rs, cols] = (cen * lax.rsqrt(var + 1e-05) * gs[h, rs, :]).astype(BF16)

    ahead = (nz - 1 - z).astype(F32)
    mine = []
    for h in range(nh):
        one = lds[h] * float(tokens * NX)
        mine.append(jnp.exp((ahead + 1.0) * one) * cb[h, 0, pl.ds(z, 1), :]
                    + jnp.exp(ahead * one) * rtot[h, pl.ds(z, 1), :])
    with jax.named_scope("fwait"):
        less = jnp.where(first, 0, jnp.where(z == 0, 2, jnp.where(z == 1, 1, 0)))
        moved_some(fr, fr_sem, nz - 1 - z - less)

        @pl.when((z == 0) & jnp.logical_not(first))
        def _():
            moved(er, er_sem).wait()

        @pl.when(z == 1)
        def _():
            moved(er.at[0], er_sem).wait()
    for h in range(nh):
        fin_ref[h] = mine[h] + jnp.sum(fr[:, h, :], axis=0, keepdims=True)

    @pl.when((z <= 1) & jnp.logical_not(first))
    def _():
        for h in range(nh):
            fin_ref[h] = fin_ref[h] + jnp.sum(er[0, :, h, :], axis=0, keepdims=True)

    @pl.when((z == 0) & jnp.logical_not(first))
    def _():
        for h in range(nh):
            fin_ref[h] = fin_ref[h] + jnp.sum(er[1, :, h, :], axis=0, keepdims=True)

    with jax.named_scope("ends"):
        less = jnp.where(last, 2, jnp.where(z == nz - 2, 1, 0))
        moved_some(fs, fs_sem, z - less + jnp.where(column & (z >= nz - 2), 1, 0))
        late = jnp.where(last, 2 * NX, jnp.where(z == nz - 2, NX, 0))
        moved_some(fs, es_sem, late - jnp.where(plane & (z >= nz - 2), 1, 0))

        @pl.when(last & jnp.logical_not(plane))
        def _():
            moved(fs, es_sem).wait()
        moved(sx.at[pl.ds(0, NX - 1)], xs_sem).wait()
        moved(cb.at[:, pl.ds(0, NX - 1)], bs_sem).wait()
        for slot, d, ok in raw:
            @pl.when(ok)
            def _(slot=slot):
                moved(rtot, as_sem.at[slot]).wait()
        for j in range(4):
            @pl.when(z + 2 + 4 * j < nz)
            def _(j=j):
                moved(win, ws_sem.at[j]).wait()


def body(table, nz, queries, key_rows, value_rows, gate_input, norm_gain):
    tokens, width = queries.shape
    nh = width // DH
    rows = DH // NX
    anyspace = pl.BlockSpec(memory_space=pl.ANY)
    vmem = pl.BlockSpec(memory_space=pltpu.VMEM)
    dma = pltpu.SemaphoreType.DMA
    wide = pltpu.VMEM((tokens, width), BF16)
    spread = pltpu.VMEM((NX, nh, rows, DH), F32)
    eight = pltpu.VMEM((nh, NX, rows, DH), F32)
    four = pltpu.VMEM((4, nh, rows, DH), F32)
    one = pltpu.VMEM((nh, rows, DH), F32)
    square = pltpu.VMEM((nh, DH, DH), F32)
    tall = pltpu.VMEM((nh, tokens, DH), F32)
    few = pltpu.VMEM((2, NX, pl.next_power_of_2(nh), DH), F32)
    line = pltpu.VMEM((nz, pl.next_power_of_2(nh), DH), F32)
    retained, final = pl.pallas_call(
        functools.partial(kernel, table, nz),
        out_shape=(pltpu.VMEM((tokens, width), BF16), pltpu.VMEM((nh, 1, DH), F32)),
        in_specs=[anyspace] * 5,
        out_specs=(vmem, vmem),
        scratch_shapes=[
            wide, wide, wide, wide, pltpu.VMEM((width,), F32),
            square, spread, spread, eight, one, four, one, four, eight, eight, square, tall, tall, line, line, few, few,
            dma((nh,)), dma((3,)), dma, dma, dma((4,)), dma((4,)), dma((4,)), dma((4,)), dma, dma((nh,)), dma, dma, dma, dma,
            pltpu.SemaphoreType.REGULAR((6,)), pltpu.SemaphoreType.REGULAR((NX,)),
        ],
        compiler_params=pltpu.CompilerParams(collective_id=0, has_side_effects=True),
        name="retention",
    )(queries, key_rows, value_rows, gate_input, norm_gain)
    return retained, final.reshape(1, nh, DH)


def solution(mesh):
    table = log_decays(mesh.shape["head"])
    rows = ("grp", "seq")
    placed = (P(rows, "head"),) * 4 + (P("head"),)
    return jax.shard_map(
        functools.partial(body, table, mesh.shape["seq"] // NX),
        mesh=mesh,
        in_specs=placed,
        out_specs=(P(rows, "head"), P(rows, "head", None)),
        check_vma=False,
    )
```

time: 61.7 us -> 57 us (0.924)
  the two profiles are of different devices: /device:TPU:66 before, /device:TPU:192 now
where the time goes in v3:
time: 57 us; the launch traced here: 56.8 us
  Pallas kernels  54.9 us (96%)
  local copies, waits for them, and re-layouts  1.28 us (2%)
  between operations  0.64 us (1%)
    pallas_call x1, Pallas kernels, body(): pl.pallas_call(functools.partial(kernel, table, nz), out_shape=(pltpu.VME...  54.9 us
    unnamed x2, local copies, waits for them, and re-layouts  1.28 us

profile of v3, /device:TPU:192, one launch (start us, length us, event | category | flops | bytes accessed | tf_op | source)
XLA Modules:
  0.0 56.8 jit_solution(5840298947107834834)
XLA Ops:
  0.6 54.9 %retention.1 = (bf16[384,384]{1,0:T(8,128)(2,1)S(1)}, f32[3,1,128]{2,1,0:T(1,128)S(1)}) custom-call(bf16[384,384]{1,0:T(8,128)(2,1)} %q_hbm.1, bf16[384,384]{1,0:T(8,128)(2,1)} %k_hbm.1, bf16[384,384]{1,0:T(8,128)(2,1)} %v_hbm.1, bf16[384,384]{1,0:T(8,128)(2,1)} %g_hbm.1, f32[384]{0:T(512)} %gain_hbm.1), custom_call_target="tpu_custom_call" | custom-call | tf_op jit(solution)/shard_map/retention/pallas_call | solution.py:524
  55.5 0.7 %copy.9 = bf16[384,384]{1,0:T(8,128)(2,1)} copy(bf16[384,384]{1,0:T(8,128)(2,1)S(1)} %get-tuple-element.6) | data formatting | bytes 589824
  56.2 0.6 copy.10

commit v4 on v3

--- a/solution.py
+++ b/solution.py
@@ -62,6 +62,9 @@
     def xwrap(d):
         return lax.rem(x + (d % NX), NX)
 
+    def r_iota(n):
+        return lax.broadcasted_iota(jnp.int32, (n, DH), 0).astype(F32)
+
     def load(src, dst, h):
         cols = pl.ds(h * DH, DH)
         return pltpu.make_async_copy(src.at[:, cols], dst.at[:, cols], kv_sem.at[h])
@@ -120,6 +123,8 @@
     count = key + z + jnp.where(last, owed + NX - 1, jnp.where(z == nz - 2, owed, 0))
     count = jnp.where((z == 0) & plane, key - 1, count)
     count = jnp.where(first, NX + nz - 3, count) - jnp.where(inner_col, 1, 0)
+    for h in range(nh):
+        inner[h] = jnp.exp((tokens - 1 - r_iota(tokens)) * lds[h]) * scale
     with jax.named_scope("barrier"):
         @pl.when(count > 0)
         def _():
@@ -145,15 +150,7 @@
     for c in whole:
         c.start()
 
-    def r_iota(n):
-        return lax.broadcasted_iota(jnp.int32, (n, DH), 0).astype(F32)
-
-    def x_copy(h, to):
-        return pltpu.make_async_remote_copy(
-            sx.at[to, h], rx.at[x, h], xs_sem, xr_sem,
-            device_id=at(z, to), device_id_type=MESH)
-
-    def x_copy_all(to):
+    def x_copy(to):
         return pltpu.make_async_remote_copy(
             sx.at[to], rx.at[x], xs_sem, xr_sem,
             device_id=at(z, to), device_id_type=MESH)
@@ -173,7 +170,7 @@
         return pltpu.make_async_copy(ref, ref, sem)
 
     def moved_some(ref, sem, n):
-        for m in range(1, ref.shape[0]):
+        for m in range(1, ref.shape[0] + 1):
             @pl.when(n == m)
             def _(m=m):
                 moved(ref.at[pl.ds(0, m)], sem).wait()
@@ -184,16 +181,14 @@
         (3, 3, z == 0),
         (2, -1, (z >= 1) & (z <= last_c + 1)),
     )
-    raw_in = ((0, (z >= 2) & (z <= last_c)), (3, z == 3), (1, (z >= 1) & (z <= last_c)), (2, z <= last_c))
-
     def a_copy(slot, d):
         return pltpu.make_async_remote_copy(
-            rtot, rz.at[slot], as_sem.at[slot], ar_sem.at[slot],
+            rtot, rz.at[slot], as_sem, ar_sem,
             device_id=at(z + d, x), device_id_type=MESH)
 
     def w_copy(j):
         return pltpu.make_async_remote_copy(
-            win, rw.at[j], ws_sem.at[j], wr_sem.at[j],
+            win, rw.at[j], ws_sem, wr_sem,
             device_id=at(z + (2 + 4 * j), x), device_id_type=MESH)
 
     def f_copy(zz):
@@ -214,18 +209,13 @@
 
     for h in range(nh):
         cols = pl.ds(h * DH, DH)
-        tail = jnp.exp((tokens - 1 - r_iota(tokens)) * lds[h]) * scale
         with jax.named_scope(f"load{h}"):
             kv_wait(h)
         with jax.named_scope(f"state{h}"):
-            kd = (k_v[:, cols].astype(F32) * tail).astype(BF16)
+            kd = (k_v[:, cols].astype(F32) * inner[h]).astype(BF16)
             st[h] = lax.dot_general(kd, v_v[:, cols], (((0,), (0,)), ((), ())), preferred_element_type=F32)
             for xx in range(NX):
                 sx[xx, h] = st[h, pl.ds(xx, rows, stride=NX), :]
-        for d in far:
-            @pl.when((key_of(xwrap(d)) < key) & (z < nz - 2))
-            def _(d=d, h=h):
-                x_copy(h, xwrap(d)).start()
 
     for r in range(nh, es.shape[2]):
         es[:, :, r, :] = jnp.zeros((2, NX, DH), F32)
@@ -246,10 +236,11 @@
                 @pl.when(ok)
                 def _(j=j, k=k, to=to):
                     e_copy(j, k, to).start()
-        for d in far:
-            @pl.when(key_of(xwrap(d)) < key)
-            def _(d=d):
-                x_copy_all(xwrap(d)).start()
+
+    for d in far:
+        @pl.when(key_of(xwrap(d)) < key)
+        def _(d=d):
+            x_copy(xwrap(d)).start()
     for d, ok in readies:
         @pl.when(ok & jnp.logical_not(column & (z == d)))
         def _(d=d):
@@ -293,7 +284,7 @@
             @pl.when((key < k) & (z == 0) & plane if k == NX else key < k)
             def _(to=to):
                 pl.semaphore_wait(xready.at[lax.rem(to + NX - x, NX)], 1)
-                x_copy_all(to).start()
+                x_copy(to).start()
 
     ri = lax.broadcasted_iota(jnp.int32, (SUB, SUB), 0)
     ci = lax.broadcasted_iota(jnp.int32, (SUB, SUB), 1)
@@ -389,10 +380,8 @@
             @pl.when(z > last_c - 2)
             def _():
                 ready_wait(2)
-            for slot, ok in raw_in:
-                @pl.when(ok)
-                def _(slot=slot):
-                    moved(rz.at[slot], ar_sem.at[slot]).wait()
+            n = 1 + jnp.where(z >= 1, 1, 0) + jnp.where(z >= 2, 1, 0) + jnp.where(z == 3, 1, 0)
+            moved_some(rz, ar_sem, n)
             for h in range(nh):
                 dd = [jnp.exp(lds[h] * float(tokens * NX * k)) for k in range(5)]
                 win[h] = (rz[2, h] + dd[1] * rtot[h] + dd[2] * rz[1, h]
@@ -400,10 +389,7 @@
             w_copy(0).start()
 
     with jax.named_scope("wwait"):
-        for j in range(4):
-            @pl.when(z >= 2 + 4 * j)
-            def _(j=j):
-                moved(rw.at[j], wr_sem.at[j]).wait()
+        moved_some(rw, wr_sem, lax.div(z + 2, 4))
 
     @pl.when(z == 1)
     def _():
@@ -489,20 +475,16 @@
         moved_some(fs, fs_sem, z - less + jnp.where(column & (z >= nz - 2), 1, 0))
         late = jnp.where(last, 2 * NX, jnp.where(z == nz - 2, NX, 0))
         moved_some(fs, es_sem, late - jnp.where(plane & (z >= nz - 2), 1, 0))
-
-        @pl.when(last & jnp.logical_not(plane))
-        def _():
-            moved(fs, es_sem).wait()
         moved(sx.at[pl.ds(0, NX - 1)], xs_sem).wait()
         moved(cb.at[:, pl.ds(0, NX - 1)], bs_sem).wait()
         for slot, d, ok in raw:
             @pl.when(ok)
             def _(slot=slot):
-                moved(rtot, as_sem.at[slot]).wait()
+                moved(rtot, as_sem).wait()
         for j in range(4):
             @pl.when(z + 2 + 4 * j < nz)
             def _(j=j):
-                moved(win, ws_sem.at[j]).wait()
+                moved(win, ws_sem).wait()
 
 
 def body(table, nz, queries, key_rows, value_rows, gate_input, norm_gain):
@@ -529,7 +511,7 @@
         scratch_shapes=[
             wide, wide, wide, wide, pltpu.VMEM((width,), F32),
             square, spread, spread, eight, one, four, one, four, eight, eight, square, tall, tall, line, line, few, few,
-            dma((nh,)), dma((3,)), dma, dma, dma((4,)), dma((4,)), dma((4,)), dma((4,)), dma, dma((nh,)), dma, dma, dma, dma,
+            dma((nh,)), dma((3,)), dma, dma, dma, dma, dma, dma, dma, dma((nh,)), dma, dma, dma, dma,
             pltpu.SemaphoreType.REGULAR((6,)), pltpu.SemaphoreType.REGULAR((NX,)),
         ],
         compiler_params=pltpu.CompilerParams(collective_id=0, has_side_effects=True),

time: 57 us -> 56.6 us (level)
  no operation moved by 1% of the time
where the time goes in v4:
time: 56.6 us; the launch traced here: 56.5 us
  Pallas kernels  54.5 us (96%)
  local copies, waits for them, and re-layouts  1.28 us (2%)
  between operations  0.64 us (1%)
    pallas_call x1, Pallas kernels, body(): pl.pallas_call(functools.partial(kernel, table, nz), out_shape=(pltpu.VME...  54.5 us
    unnamed x2, local copies, waits for them, and re-layouts  1.28 us

profile of v4, /device:TPU:192, one launch (start us, length us, event | category | flops | bytes accessed | tf_op | source)
XLA Modules:
  0.0 56.5 jit_solution(11119791120317871719)
XLA Ops:
  0.6 54.5 %retention.1 = (bf16[384,384]{1,0:T(8,128)(2,1)S(1)}, f32[3,1,128]{2,1,0:T(1,128)S(1)}) custom-call(bf16[384,384]{1,0:T(8,128)(2,1)} %q_hbm.1, bf16[384,384]{1,0:T(8,128)(2,1)} %k_hbm.1, bf16[384,384]{1,0:T(8,128)(2,1)} %v_hbm.1, bf16[384,384]{1,0:T(8,128)(2,1)} %g_hbm.1, f32[384]{0:T(512)} %gain_hbm.1), custom_call_target="tpu_custom_call" | custom-call | tf_op jit(solution)/shard_map/retention/pallas_call | solution.py:506
  55.2 0.7 %copy.9 = bf16[384,384]{1,0:T(8,128)(2,1)} copy(bf16[384,384]{1,0:T(8,128)(2,1)S(1)} %get-tuple-element.6) | data formatting | bytes 589824
  55.9 0.6 copy.10

commit v5 on v4

--- a/solution.py
+++ b/solution.py
@@ -46,7 +46,7 @@
     plane = (lax.axis_index("grp") == 0) & (hd == 0)
     column = plane & (x == 0)
     first = column & (z == 0)
-    inner_col = column & (z > 0) & (z < nz - 1)
+    inner_col = column & (z > 0) & (z < nz - 2)
     last_c = nz - 3
 
     lds = []
@@ -79,17 +79,16 @@
         pltpu.make_async_copy(gain_hbm, gain_v, in_sem.at[2]),
     )
 
-    for h in range(nh):
-        load(k_hbm, k_v, h).start()
-        load(v_hbm, v_v, h).start()
-
     def key_of(xx):
         k = jnp.where(xx < NX // 2, xx, 3 * NX // 2 - 1 - xx)
+        k = jnp.where(xx == NX // 2, NX - 2, jnp.where(xx == NX // 2 + 1, NX - 1, k))
         return jnp.where((xx == 0) & (z == 0) & plane, NX, k)
 
     def x_of(k):
         if k == NX:
             return 0
+        if k >= NX - 2:
+            return k - NX // 2 + 2
         return k if k < NX // 2 else 3 * NX // 2 - 1 - k
 
     key = key_of(x)
@@ -99,13 +98,17 @@
         @pl.when(key_of(xwrap(d)) > key)
         def _(d=d):
             pl.semaphore_signal(barrier, inc=1, device_id=at(z, xwrap(d)), device_id_type=MESH)
+    for h in range(nh):
+        load(k_hbm, k_v, h).start()
+        load(v_hbm, v_v, h).start()
+
     last = z == nz - 1
-    express = ((0, 0), (1, 0), (0, 1))
+    express = ((0, 0), (1, 0), (0, 1), (0, 2))
 
     def tell_later():
         for zz in range(1, nz):
             ok = z < zz
-            if zz < nz - 1:
+            if zz < nz - 2:
                 ok = ok & jnp.logical_not(first)
 
             @pl.when(ok)
@@ -120,9 +123,9 @@
     def _():
         pl.semaphore_signal(barrier, inc=1, device_id=at(0, x), device_id_type=MESH)
     owed = jnp.where(plane, NX - 1 - jnp.where(x == 0, 0, 1), NX - 1)
-    count = key + z + jnp.where(last, owed + NX - 1, jnp.where(z == nz - 2, owed, 0))
+    count = key + z + jnp.where(last, owed + NX - 1, jnp.where((z == nz - 2) | (z == nz - 3), owed, 0))
     count = jnp.where((z == 0) & plane, key - 1, count)
-    count = jnp.where(first, NX + nz - 3, count) - jnp.where(inner_col, 1, 0)
+    count = jnp.where(first, NX + nz - 4, count) - jnp.where(inner_col, 1, 0)
     for h in range(nh):
         inner[h] = jnp.exp((tokens - 1 - r_iota(tokens)) * lds[h]) * scale
     with jax.named_scope("barrier"):
@@ -140,7 +143,7 @@
 
     @pl.when(first)
     def _():
-        for zz in range(1, nz - 1):
+        for zz in range(1, nz - 2):
             pl.semaphore_signal(xready.at[0], inc=1, device_id=at(zz, x), device_id_type=MESH)
     for j, k in express:
         @pl.when((z == j) & jnp.logical_not(first))
@@ -201,7 +204,7 @@
     slot_of = {d: i for i, (d, _) in enumerate(readies)}
 
     def ready_wait(d):
-        @pl.when(jnp.logical_not(first))
+        @pl.when(jnp.logical_not(first) if d < nz - 2 else z >= 0)
         def _():
             pl.semaphore_wait(ready.at[slot_of[d]], 1)
 
@@ -220,7 +223,7 @@
     for r in range(nh, es.shape[2]):
         es[:, :, r, :] = jnp.zeros((2, NX, DH), F32)
 
-    @pl.when(z >= nz - 2)
+    @pl.when(z >= nz - 3)
     def _():
         for h in range(nh):
             w = (NX - 1 - x + NX * (nz - 1 - z)).astype(F32) * (lds[h] * float(tokens))
@@ -242,7 +245,7 @@
         def _(d=d):
             x_copy(xwrap(d)).start()
     for d, ok in readies:
-        @pl.when(ok & jnp.logical_not(column & (z == d)))
+        @pl.when(ok & jnp.logical_not(inner_col & (z == d)))
         def _(d=d):
             pl.semaphore_signal(ready.at[slot_of[d]], inc=1, device_id=at(z - d, x), device_id_type=MESH)
 
@@ -422,23 +425,37 @@
     def _():
         local_work()
 
-    for h in range(nh):
+    def outer_of(h):
         cols = pl.ds(h * DH, DH)
         lead = jnp.exp((r_iota(SUB) + 1.0) * lds[h])
+        for xx in range(NX):
+            carr[h, pl.ds(xx, rows, stride=NX), :] = rc[h, xx]
+        low = carr[h].astype(BF16)
+        o = jnp.dot(q_v[:, cols], low, preferred_element_type=F32)
+        for i in range(nb):
+            rs = pl.ds(i * SUB, SUB)
+            inner[h, rs, :] = (inner[h, rs, :]
+                               + o[i * SUB:(i + 1) * SUB] * (lead * jnp.exp(lds[h] * float(i * SUB))))
+
+    def norm_of(h):
+        cols = pl.ds(h * DH, DH)
+        for i in range(nb):
+            rs = pl.ds(i * SUB, SUB)
+            mix = inner[h, rs, :]
+            mean = jnp.sum(mix, axis=1, keepdims=True) * (1.0 / DH)
+            cen = mix - mean
+            var = jnp.sum(cen * cen, axis=1, keepdims=True) * (1.0 / DH)
+            out_ref[rs, cols] = (cen * lax.rsqrt(var + 1e-05) * gs[h, rs, :]).astype(BF16)
+
+    for h in range(nh):
         with jax.named_scope(f"bwait{h}"):
             moved(rc.at[h, pl.ds(0, NX - 1)], br_sem.at[h]).wait()
         with jax.named_scope(f"outer{h}"):
-            for xx in range(NX):
-                carr[h, pl.ds(xx, rows, stride=NX), :] = rc[h, xx]
-            low = carr[h].astype(BF16)
-            for i in range(nb):
-                rs = pl.ds(i * SUB, SUB)
-                o = jnp.dot(q_v[rs, cols], low, preferred_element_type=F32)
-                mix = inner[h, rs, :] + o * (lead * jnp.exp(lds[h] * float(i * SUB)))
-                mean = jnp.sum(mix, axis=1, keepdims=True) * (1.0 / DH)
-                cen = mix - mean
-                var = jnp.sum(cen * cen, axis=1, keepdims=True) * (1.0 / DH)
-                out_ref[rs, cols] = (cen * lax.rsqrt(var + 1e-05) * gs[h, rs, :]).astype(BF16)
+            outer_of(h)
+            if h > 0:
+                norm_of(h - 1)
+    with jax.named_scope("norm"):
+        norm_of(nh - 1)
 
     ahead = (nz - 1 - z).astype(F32)
     mine = []
@@ -447,7 +464,7 @@
         mine.append(jnp.exp((ahead + 1.0) * one) * cb[h, 0, pl.ds(z, 1), :]
                     + jnp.exp(ahead * one) * rtot[h, pl.ds(z, 1), :])
     with jax.named_scope("fwait"):
-        less = jnp.where(first, 0, jnp.where(z == 0, 2, jnp.where(z == 1, 1, 0)))
+        less = jnp.where(first, 0, jnp.where(z == 0, 3, jnp.where(z == 1, 1, 0)))
         moved_some(fr, fr_sem, nz - 1 - z - less)
 
         @pl.when((z == 0) & jnp.logical_not(first))
@@ -468,13 +485,14 @@
     @pl.when((z == 0) & jnp.logical_not(first))
     def _():
         for h in range(nh):
-            fin_ref[h] = fin_ref[h] + jnp.sum(er[1, :, h, :], axis=0, keepdims=True)
+            for k in range(1, 3):
+                fin_ref[h] = fin_ref[h] + jnp.sum(er[k, :, h, :], axis=0, keepdims=True)
 
     with jax.named_scope("ends"):
-        less = jnp.where(last, 2, jnp.where(z == nz - 2, 1, 0))
-        moved_some(fs, fs_sem, z - less + jnp.where(column & (z >= nz - 2), 1, 0))
-        late = jnp.where(last, 2 * NX, jnp.where(z == nz - 2, NX, 0))
-        moved_some(fs, es_sem, late - jnp.where(plane & (z >= nz - 2), 1, 0))
+        less = jnp.where(last, 2, jnp.where(z >= nz - 3, 1, 0))
+        moved_some(fs, fs_sem, z - less + jnp.where(column & (z >= nz - 3), 1, 0))
+        late = jnp.where(last, 2 * NX, jnp.where(z >= nz - 3, NX, 0))
+        moved_some(fs, es_sem, late - jnp.where(plane & (z >= nz - 3), 1, 0))
         moved(sx.at[pl.ds(0, NX - 1)], xs_sem).wait()
         moved(cb.at[:, pl.ds(0, NX - 1)], bs_sem).wait()
         for slot, d, ok in raw:
@@ -485,6 +503,15 @@
             @pl.when(z + 2 + 4 * j < nz)
             def _(j=j):
                 moved(win, ws_sem).wait()
+
+
+def put(a_ref, b_ref, a_out, b_out, sem):
+    one = pltpu.make_async_copy(a_ref, a_out, sem.at[0])
+    two = pltpu.make_async_copy(b_ref, b_out, sem.at[1])
+    one.start()
+    two.start()
+    one.wait()
+    two.wait()
 
 
 def body(table, nz, queries, key_rows, value_rows, gate_input, norm_gain):
@@ -501,7 +528,7 @@
     one = pltpu.VMEM((nh, rows, DH), F32)
     square = pltpu.VMEM((nh, DH, DH), F32)
     tall = pltpu.VMEM((nh, tokens, DH), F32)
-    few = pltpu.VMEM((2, NX, pl.next_power_of_2(nh), DH), F32)
+    few = pltpu.VMEM((3, NX, pl.next_power_of_2(nh), DH), F32)
     line = pltpu.VMEM((nz, pl.next_power_of_2(nh), DH), F32)
     retained, final = pl.pallas_call(
         functools.partial(kernel, table, nz),
@@ -510,13 +537,22 @@
         out_specs=(vmem, vmem),
         scratch_shapes=[
             wide, wide, wide, wide, pltpu.VMEM((width,), F32),
-            square, spread, spread, eight, one, four, one, four, eight, eight, square, tall, tall, line, line, few, few,
+            square, spread, spread, eight, one, four, one, four, eight, eight, square, tall, tall, line, line, pltpu.VMEM((2, NX, pl.next_power_of_2(nh), DH), F32), few,
             dma((nh,)), dma((3,)), dma, dma, dma, dma, dma, dma, dma, dma((nh,)), dma, dma, dma, dma,
             pltpu.SemaphoreType.REGULAR((6,)), pltpu.SemaphoreType.REGULAR((NX,)),
         ],
         compiler_params=pltpu.CompilerParams(collective_id=0, has_side_effects=True),
         name="retention",
     )(queries, key_rows, value_rows, gate_input, norm_gain)
+    retained, final = (pltpu.with_memory_space_constraint(a, pltpu.VMEM) for a in (retained, final))
+    retained, final = pl.pallas_call(
+        put,
+        out_shape=(jax.ShapeDtypeStruct((tokens, width), BF16), jax.ShapeDtypeStruct((nh, 1, DH), F32)),
+        in_specs=[vmem, vmem],
+        out_specs=(anyspace, anyspace),
+        scratch_shapes=[dma((2,))],
+        name="put",
+    )(retained, final)
     return retained, final.reshape(1, nh, DH)
 
 

time: 56.6 us -> 55.9 us (0.988)
  local copies, waits for them, and re-layouts: 1.28 us -> 0 us
  Pallas kernels: 54.5 us -> 55.1 us
    unnamed x2 -> x0, local copies, waits for them, and re-layouts: 1.28 us -> none
    pallas_call x0 -> x1, Pallas kernels: none -> 0.74 us  [body(): pl.pallas_call(put, out_shape=(jax.ShapeDtypeStruct((tokens, width), BF16...]
where the time goes in v5:
time: 55.9 us; the launch traced here: 55.7 us
  Pallas kernels  55.1 us (99%)
  between operations  0.64 us (1%)
    pallas_call x1, Pallas kernels, body(): pl.pallas_call(functools.partial(kernel, table, nz), out_shape=(pltpu.VME...  54.3 us

profile of v5, /device:TPU:192, one launch (start us, length us, event | category | flops | bytes accessed | tf_op | source)
XLA Modules:
  0.0 55.7 jit_solution(1050222732812464062)
XLA Ops:
  0.6 54.3 %retention.1 = (bf16[384,384]{1,0:T(8,128)(2,1)S(1)}, f32[3,1,128]{2,1,0:T(1,128)S(1)}) custom-call(bf16[384,384]{1,0:T(8,128)(2,1)} %q_hbm.1, bf16[384,384]{1,0:T(8,128)(2,1)} %k_hbm.1, bf16[384,384]{1,0:T(8,128)(2,1)} %v_hbm.1, bf16[384,384]{1,0:T(8,128)(2,1)} %g_hbm.1, f32[384]{0:T(512)} %gain_hbm.1), custom_call_target="tpu_custom_call" | custom-call | tf_op jit(solution)/shard_map/retention/pallas_call | solution.py:533
  55.0 0.7 %put.1 = (bf16[384,384]{1,0:T(8,128)(2,1)}, f32[3,1,128]{2,1,0:T(1,128)}) custom-call(bf16[384,384]{1,0:T(8,128)(2,1)S(1)} %get-tuple-element.6.a_ref, f32[3,1,128]{2,1,0:T(1,128)S(1)} %get-tuple-element.7.b_ref), custom_call_target="tpu_custom_call" | custom-call | tf_op jit(solution)/shard_map/put/pallas_call | solution.py:548

commit v6 on v5

--- a/solution.py
+++ b/solution.py
@@ -31,8 +31,8 @@
     q_hbm, k_hbm, v_hbm, g_hbm, gain_hbm,
     out_ref, fin_ref,
     q_v, k_v, v_v, g_v, gain_v,
-    st, sx, rx, xp, rtot, rz, win, rw, cb, rc, carr, inner, gs, fs, fr, es, er,
-    kv_sem, in_sem, xs_sem, xr_sem, as_sem, ar_sem, ws_sem, wr_sem, bs_sem, br_sem, fs_sem, fr_sem, es_sem, er_sem, ready, xready,
+    st, sx, rx, xp, rtot, rz, win, rw, cb, rc, carr, inner, gs, fs, fr, es, er, r2, cb2,
+    kv_sem, in_sem, xs_sem, xr_sem, ar_sem, wr_sem, br_sem, fr_sem, er_sem, r2_sem, ready, xready, two,
 ):
     tokens = q_v.shape[0]
     nh = q_v.shape[1] // DH
@@ -46,6 +46,8 @@
     plane = (lax.axis_index("grp") == 0) & (hd == 0)
     column = plane & (x == 0)
     first = column & (z == 0)
+    row0 = plane & (z == 0)
+    row1 = plane & (z == 1)
     inner_col = column & (z > 0) & (z < nz - 2)
     last_c = nz - 3
 
@@ -79,6 +81,10 @@
         pltpu.make_async_copy(gain_hbm, gain_v, in_sem.at[2]),
     )
 
+    for h in range(nh):
+        load(k_hbm, k_v, h).start()
+        load(v_hbm, v_v, h).start()
+
     def key_of(xx):
         k = jnp.where(xx < NX // 2, xx, 3 * NX // 2 - 1 - xx)
         k = jnp.where(xx == NX // 2, NX - 2, jnp.where(xx == NX // 2 + 1, NX - 1, k))
@@ -98,12 +104,8 @@
         @pl.when(key_of(xwrap(d)) > key)
         def _(d=d):
             pl.semaphore_signal(barrier, inc=1, device_id=at(z, xwrap(d)), device_id_type=MESH)
-    for h in range(nh):
-        load(k_hbm, k_v, h).start()
-        load(v_hbm, v_v, h).start()
-
     last = z == nz - 1
-    express = ((0, 0), (1, 0), (0, 1), (0, 2))
+    express = ((0, 0), (1, 0), (0, 1), (0, 2), (1, 1))
 
     def tell_later():
         for zz in range(1, nz):
@@ -122,10 +124,14 @@
     @pl.when(inner_col)
     def _():
         pl.semaphore_signal(barrier, inc=1, device_id=at(0, x), device_id_type=MESH)
+
+    @pl.when(row1 & (x > 0))
+    def _():
+        pl.semaphore_signal(barrier, inc=1, device_id=at(0, 0), device_id_type=MESH)
     owed = jnp.where(plane, NX - 1 - jnp.where(x == 0, 0, 1), NX - 1)
-    count = key + z + jnp.where(last, owed + NX - 1, jnp.where((z == nz - 2) | (z == nz - 3), owed, 0))
+    count = key + z + jnp.where(z >= nz - 2, owed + NX - 1, jnp.where((z == nz - 3) | row1, owed, 0))
     count = jnp.where((z == 0) & plane, key - 1, count)
-    count = jnp.where(first, NX + nz - 4, count) - jnp.where(inner_col, 1, 0)
+    count = jnp.where(first, 2 * NX + nz - 5, count) - jnp.where(inner_col, 1, 0)
     for h in range(nh):
         inner[h] = jnp.exp((tokens - 1 - r_iota(tokens)) * lds[h]) * scale
     with jax.named_scope("barrier"):
@@ -145,6 +151,14 @@
     def _():
         for zz in range(1, nz - 2):
             pl.semaphore_signal(xready.at[0], inc=1, device_id=at(zz, x), device_id_type=MESH)
+    @pl.when(row0 & jnp.logical_not(first))
+    def _():
+        for d in range(1, NX):
+            pl.semaphore_signal(barrier, inc=1, device_id=at(1, xwrap(d)), device_id_type=MESH)
+    for to in range(1, NX):
+        @pl.when(row1)
+        def _(to=to):
+            pl.semaphore_signal(two, inc=1, device_id=at(0, to), device_id_type=MESH)
     for j, k in express:
         @pl.when((z == j) & jnp.logical_not(first))
         def _(k=k):
@@ -159,14 +173,26 @@
             device_id=at(z, to), device_id_type=MESH)
 
     def b_copy(h, d):
-        to = xwrap(d)
-        return pltpu.make_async_remote_copy(
-            cb.at[h, to], rc.at[h, x], bs_sem, br_sem.at[h],
+        return b_to(h, xwrap(d))
+
+    def b_to(h, to):
+        return pltpu.make_async_remote_copy(
+            cb.at[h, to], rc.at[h, x], xs_sem, br_sem.at[h],
             device_id=at(z, to), device_id_type=MESH)
 
+    def d_copy(to):
+        return pltpu.make_async_remote_copy(
+            sx.at[to], r2.at[x], xs_sem, r2_sem,
+            device_id=at(1, to), device_id_type=MESH)
+
+    def s_copy(h, to):
+        return pltpu.make_async_remote_copy(
+            cb2.at[h, to], rc.at[h, 0], xs_sem, br_sem.at[h],
+            device_id=at(0, to), device_id_type=MESH)
+
     def e_copy(j, k, to):
         return pltpu.make_async_remote_copy(
-            es.at[j, to], er.at[k, x], es_sem, er_sem,
+            es.at[j, to], er.at[k, x], xs_sem, er_sem,
             device_id=at(j, to), device_id_type=MESH)
 
     def moved(ref, sem):
@@ -179,24 +205,24 @@
                 moved(ref.at[pl.ds(0, m)], sem).wait()
 
     raw = (
-        (1, 1, z <= last_c - 1),
+        (1, 1, (z <= last_c - 1) & jnp.logical_not(row0)),
         (0, 2, z <= last_c - 2),
         (3, 3, z == 0),
         (2, -1, (z >= 1) & (z <= last_c + 1)),
     )
     def a_copy(slot, d):
         return pltpu.make_async_remote_copy(
-            rtot, rz.at[slot], as_sem, ar_sem,
+            rtot, rz.at[slot], xs_sem, ar_sem,
             device_id=at(z + d, x), device_id_type=MESH)
 
     def w_copy(j):
         return pltpu.make_async_remote_copy(
-            win, rw.at[j], ws_sem, wr_sem,
+            win, rw.at[j], xs_sem, wr_sem,
             device_id=at(z + (2 + 4 * j), x), device_id_type=MESH)
 
     def f_copy(zz):
         return pltpu.make_async_remote_copy(
-            fs.at[zz], fr.at[z], fs_sem, fr_sem,
+            fs.at[zz], fr.at[z], xs_sem, fr_sem,
             device_id=at(zz, x), device_id_type=MESH)
 
     readies = ((1, (z >= 1) & (z <= last_c)), (2, z >= 2), (3, z == 3)) + tuple(
@@ -210,11 +236,12 @@
 
     far = (4, 3, 5, 2, 6, 1, 7)
 
-    for h in range(nh):
-        cols = pl.ds(h * DH, DH)
-        with jax.named_scope(f"load{h}"):
+    with jax.named_scope("load"):
+        for h in range(nh):
             kv_wait(h)
-        with jax.named_scope(f"state{h}"):
+    with jax.named_scope("state"):
+        for h in range(nh):
+            cols = pl.ds(h * DH, DH)
             kd = (k_v[:, cols].astype(F32) * inner[h]).astype(BF16)
             st[h] = lax.dot_general(kd, v_v[:, cols], (((0,), (0,)), ((), ())), preferred_element_type=F32)
             for xx in range(NX):
@@ -240,12 +267,18 @@
                 def _(j=j, k=k, to=to):
                     e_copy(j, k, to).start()
 
+    @pl.when(first)
+    def _():
+        for d in far:
+            x_copy(xwrap(d)).start()
+            d_copy(xwrap(d)).start()
+        d_copy(x).start()
     for d in far:
-        @pl.when(key_of(xwrap(d)) < key)
+        @pl.when((key_of(xwrap(d)) < key) & jnp.logical_not(first))
         def _(d=d):
             x_copy(xwrap(d)).start()
     for d, ok in readies:
-        @pl.when(ok & jnp.logical_not(inner_col & (z == d)))
+        @pl.when(ok & jnp.logical_not((plane if d == 1 else inner_col) & (z == d)))
         def _(d=d):
             pl.semaphore_signal(ready.at[slot_of[d]], inc=1, device_id=at(z - d, x), device_id_type=MESH)
 
@@ -280,6 +313,12 @@
     for r in range(nh, fs.shape[1]):
         fs[:, r, :] = jnp.zeros((nz, DH), F32)
     rx[x] = sx[x]
+
+    @pl.when(row0 & jnp.logical_not(first))
+    def _():
+        pl.semaphore_wait(two, NX)
+        for d in far + (0,):
+            d_copy(xwrap(d)).start()
     with jax.named_scope("xready"):
         for k in range(1, NX + 1):
             to = x_of(k)
@@ -369,13 +408,35 @@
             cb[h, 0] = jnp.zeros((rows, DH), F32)
             for xx in range(1, NX):
                 cb[h, xx] = xp[h, xx]
-            back(h)
+            rc[h, x] = cb[h, x]
+        for to in (1, 2, 3, 7, 6, 5, 4, 0):
+            @pl.when((x != to) & jnp.logical_not(first))
+            def _(to=to):
+                for h in range(nh):
+                    b_to(h, to).start()
 
     early = (z >= 1) & (z < nz // 2)
 
     @pl.when(early)
     def _():
         local_work()
+
+    @pl.when(row1)
+    def _():
+        with jax.named_scope("row0"):
+            moved(r2, r2_sem).wait()
+            for h in range(nh):
+                d1 = jnp.exp(lds[h] * float(tokens))
+                acc = r2[0, h]
+                for xx in range(1, NX):
+                    cb2[h, xx] = acc
+                    acc = acc * d1 + r2[xx, h]
+                rz[1, h] = acc
+
+                @pl.when(x == 0)
+                def _(h=h):
+                    for to in (4, 5, 3, 6, 2, 7, 1):
+                        s_copy(h, to).start()
 
     @pl.when(z <= last_c)
     def _():
@@ -383,7 +444,7 @@
             @pl.when(z > last_c - 2)
             def _():
                 ready_wait(2)
-            n = 1 + jnp.where(z >= 1, 1, 0) + jnp.where(z >= 2, 1, 0) + jnp.where(z == 3, 1, 0)
+            n = 1 + jnp.where((z >= 1) & jnp.logical_not(row1), 1, 0) + jnp.where(z >= 2, 1, 0) + jnp.where(z == 3, 1, 0)
             moved_some(rz, ar_sem, n)
             for h in range(nh):
                 dd = [jnp.exp(lds[h] * float(tokens * NX * k)) for k in range(5)]
@@ -464,7 +525,7 @@
         mine.append(jnp.exp((ahead + 1.0) * one) * cb[h, 0, pl.ds(z, 1), :]
                     + jnp.exp(ahead * one) * rtot[h, pl.ds(z, 1), :])
     with jax.named_scope("fwait"):
-        less = jnp.where(first, 0, jnp.where(z == 0, 3, jnp.where(z == 1, 1, 0)))
+        less = jnp.where(first, 0, jnp.where(z == 0, 3, jnp.where(z == 1, 2, 0)))
         moved_some(fr, fr_sem, nz - 1 - z - less)
 
         @pl.when((z == 0) & jnp.logical_not(first))
@@ -473,36 +534,47 @@
 
         @pl.when(z == 1)
         def _():
-            moved(er.at[0], er_sem).wait()
+            moved(er.at[pl.ds(0, 2)], er_sem).wait()
     for h in range(nh):
         fin_ref[h] = mine[h] + jnp.sum(fr[:, h, :], axis=0, keepdims=True)
 
     @pl.when((z <= 1) & jnp.logical_not(first))
     def _():
         for h in range(nh):
-            fin_ref[h] = fin_ref[h] + jnp.sum(er[0, :, h, :], axis=0, keepdims=True)
+            for k in range(2):
+                fin_ref[h] = fin_ref[h] + jnp.sum(er[k, :, h, :], axis=0, keepdims=True)
 
     @pl.when((z == 0) & jnp.logical_not(first))
     def _():
         for h in range(nh):
-            for k in range(1, 3):
-                fin_ref[h] = fin_ref[h] + jnp.sum(er[k, :, h, :], axis=0, keepdims=True)
+            fin_ref[h] = fin_ref[h] + jnp.sum(er[2, :, h, :], axis=0, keepdims=True)
 
     with jax.named_scope("ends"):
-        less = jnp.where(last, 2, jnp.where(z >= nz - 3, 1, 0))
-        moved_some(fs, fs_sem, z - less + jnp.where(column & (z >= nz - 3), 1, 0))
-        late = jnp.where(last, 2 * NX, jnp.where(z >= nz - 3, NX, 0))
-        moved_some(fs, es_sem, late - jnp.where(plane & (z >= nz - 3), 1, 0))
+        less = jnp.where(z >= nz - 2, 2, jnp.where(z == nz - 3, 1, 0))
+        moved_some(fs, xs_sem, z - less + jnp.where(column & (z >= nz - 3), 1, 0))
+        late = jnp.where(z >= nz - 2, 2 * NX, jnp.where(z == nz - 3, NX, 0))
+        moved_some(fs, xs_sem, late - jnp.where(plane & (z >= nz - 3), 1, 0))
         moved(sx.at[pl.ds(0, NX - 1)], xs_sem).wait()
-        moved(cb.at[:, pl.ds(0, NX - 1)], bs_sem).wait()
+
+        @pl.when(row0)
+        def _():
+            moved(sx, xs_sem).wait()
+
+        @pl.when(jnp.logical_not(first))
+        def _():
+            moved(cb.at[:, pl.ds(0, NX - 1)], xs_sem).wait()
+
+        @pl.when(row1 & (x == 0))
+        def _():
+            moved(cb2.at[:, pl.ds(0, NX - 1)], xs_sem).wait()
         for slot, d, ok in raw:
             @pl.when(ok)
             def _(slot=slot):
-                moved(rtot, as_sem).wait()
+                moved(rtot, xs_sem).wait()
         for j in range(4):
             @pl.when(z + 2 + 4 * j < nz)
             def _(j=j):
-                moved(win, ws_sem).wait()
+                moved(win, xs_sem).wait()
 
 
 def put(a_ref, b_ref, a_out, b_out, sem):
@@ -537,9 +609,11 @@
         out_specs=(vmem, vmem),
         scratch_shapes=[
             wide, wide, wide, wide, pltpu.VMEM((width,), F32),
-            square, spread, spread, eight, one, four, one, four, eight, eight, square, tall, tall, line, line, pltpu.VMEM((2, NX, pl.next_power_of_2(nh), DH), F32), few,
-            dma((nh,)), dma((3,)), dma, dma, dma, dma, dma, dma, dma, dma((nh,)), dma, dma, dma, dma,
+            square, spread, spread, eight, one, four, one, four, eight, eight, square, tall, tall, line, line,
+            pltpu.VMEM((2, NX, pl.next_power_of_2(nh), DH), F32), few, spread, eight,
+            dma((nh,)), dma((3,)), dma, dma, dma, dma, dma((nh,)), dma, dma, dma,
             pltpu.SemaphoreType.REGULAR((6,)), pltpu.SemaphoreType.REGULAR((NX,)),
+            pltpu.SemaphoreType.REGULAR,
         ],
         compiler_params=pltpu.CompilerParams(collective_id=0, has_side_effects=True),
         name="retention",

time: 55.9 us -> 54.7 us (0.979)
  the two profiles are of different devices: /device:TPU:192 before, /device:TPU:66 now
where the time goes in v6:
time: 54.7 us; the launch traced here: 54.6 us
  Pallas kernels  53.9 us (99%)
  between operations  0.64 us (1%)
    pallas_call x1, Pallas kernels, body(): pl.pallas_call(functools.partial(kernel, table, nz), out_shape=(pltpu.VME...  53.2 us

profile of v6, /device:TPU:66, one launch (start us, length us, event | category | flops | bytes accessed | tf_op | source)
XLA Modules:
  0.0 54.6 jit_solution(15387689530178903795)
XLA Ops:
  0.6 53.2 %retention.1 = (bf16[384,384]{1,0:T(8,128)(2,1)S(1)}, f32[3,1,128]{2,1,0:T(1,128)S(1)}) custom-call(bf16[384,384]{1,0:T(8,128)(2,1)} %q_hbm.1, bf16[384,384]{1,0:T(8,128)(2,1)} %k_hbm.1, bf16[384,384]{1,0:T(8,128)(2,1)} %v_hbm.1, bf16[384,384]{1,0:T(8,128)(2,1)} %g_hbm.1, f32[384]{0:T(512)} %gain_hbm.1), custom_call_target="tpu_custom_call" | custom-call | tf_op jit(solution)/shard_map/retention/pallas_call | solution.py:605
  53.8 0.7 %put.1 = (bf16[384,384]{1,0:T(8,128)(2,1)}, f32[3,1,128]{2,1,0:T(1,128)}) custom-call(bf16[384,384]{1,0:T(8,128)(2,1)S(1)} %get-tuple-element.6.a_ref, f32[3,1,128]{2,1,0:T(1,128)S(1)} %get-tuple-element.7.b_ref), custom_call_target="tpu_custom_call" | custom-call | tf_op jit(solution)/shard_map/put/pallas_call | solution.py:622

commit v7 on v6

--- a/solution.py
+++ b/solution.py
@@ -164,9 +164,6 @@
         def _(k=k):
             for d in range(1, NX):
                 pl.semaphore_signal(barrier, inc=1, device_id=at(nz - 1 - k, xwrap(d)), device_id_type=MESH)
-    for c in whole:
-        c.start()
-
     def x_copy(to):
         return pltpu.make_async_remote_copy(
             sx.at[to], rx.at[x], xs_sem, xr_sem,
@@ -281,6 +278,8 @@
         @pl.when(ok & jnp.logical_not((plane if d == 1 else inner_col) & (z == d)))
         def _(d=d):
             pl.semaphore_signal(ready.at[slot_of[d]], inc=1, device_id=at(z - d, x), device_id_type=MESH)
+    for c in whole:
+        c.start()
 
     zero = jnp.zeros((nh, rows, DH), F32)
 
@@ -373,7 +372,25 @@
                 xp[h, xx] = acc
                 acc = acc * d1 + rx[xx, h]
             rtot[h] = acc
-            fs[:, h, :] = acc * jnp.exp((nz - 1 - z).astype(F32) * (lds[h] * float(tokens * NX)))
+
+    @pl.when(z == 0)
+    def _():
+        for h in range(nh):
+            xp[h, 0] = jnp.zeros((rows, DH), F32)
+            cb[h, 0] = jnp.zeros((rows, DH), F32)
+            rc[h, x] = xp[h, x]
+        for to in (1, 2, 3, 7, 6, 5, 4, 0):
+            @pl.when((x != to) & jnp.logical_not(first))
+            def _(to=to):
+                for h in range(nh):
+                    pltpu.make_async_remote_copy(
+                        xp.at[h, to], rc.at[h, x], xs_sem, br_sem.at[h],
+                        device_id=at(z, to), device_id_type=MESH).start()
+
+    @pl.when(z > 0)
+    def _():
+        for h in range(nh):
+            fs[:, h, :] = rtot[h] * jnp.exp((nz - 1 - z).astype(F32) * (lds[h] * float(tokens * NX)))
 
     for zz in range(nz - 1):
         ok = z > zz
@@ -402,19 +419,6 @@
             b_copy(h, d).start()
         rc[h, x] = cb[h, x]
 
-    @pl.when(z == 0)
-    def _():
-        for h in range(nh):
-            cb[h, 0] = jnp.zeros((rows, DH), F32)
-            for xx in range(1, NX):
-                cb[h, xx] = xp[h, xx]
-            rc[h, x] = cb[h, x]
-        for to in (1, 2, 3, 7, 6, 5, 4, 0):
-            @pl.when((x != to) & jnp.logical_not(first))
-            def _(to=to):
-                for h in range(nh):
-                    b_to(h, to).start()
-
     early = (z >= 1) & (z < nz // 2)
 
     @pl.when(early)
@@ -433,9 +437,10 @@
                     acc = acc * d1 + r2[xx, h]
                 rz[1, h] = acc
 
-                @pl.when(x == 0)
-                def _(h=h):
-                    for to in (4, 5, 3, 6, 2, 7, 1):
+            @pl.when(x == 0)
+            def _():
+                for to in (1, 2, 3, 7, 6, 5, 4):
+                    for h in range(nh):
                         s_copy(h, to).start()
 
     @pl.when(z <= last_c)

time: 54.7 us -> 54.6 us (level)
  no operation moved by 1% of the time
where the time goes in v7:
time: 54.6 us; the launch traced here: 54.4 us
  Pallas kernels  53.8 us (99%)
  between operations  0.64 us (1%)
    pallas_call x1, Pallas kernels, body(): pl.pallas_call(functools.partial(kernel, table, nz), out_shape=(pltpu.VME...  53 us

profile of v7, /device:TPU:66, one launch (start us, length us, event | category | flops | bytes accessed | tf_op | source)
XLA Modules:
  0.0 54.4 jit_solution(8058036661869867299)
XLA Ops:
  0.6 53.0 %retention.1 = (bf16[384,384]{1,0:T(8,128)(2,1)S(1)}, f32[3,1,128]{2,1,0:T(1,128)S(1)}) custom-call(bf16[384,384]{1,0:T(8,128)(2,1)} %q_hbm.1, bf16[384,384]{1,0:T(8,128)(2,1)} %k_hbm.1, bf16[384,384]{1,0:T(8,128)(2,1)} %v_hbm.1, bf16[384,384]{1,0:T(8,128)(2,1)} %g_hbm.1, f32[384]{0:T(512)} %gain_hbm.1), custom_call_target="tpu_custom_call" | custom-call | tf_op jit(solution)/shard_map/retention/pallas_call | solution.py:610
  53.7 0.7 %put.1 = (bf16[384,384]{1,0:T(8,128)(2,1)}, f32[3,1,128]{2,1,0:T(1,128)}) custom-call(bf16[384,384]{1,0:T(8,128)(2,1)S(1)} %get-tuple-element.6.a_ref, f32[3,1,128]{2,1,0:T(1,128)S(1)} %get-tuple-element.7.b_ref), custom_call_target="tpu_custom_call" | custom-call | tf_op jit(solution)/shard_map/put/pallas_call | solution.py:627

commit v8 on v7

--- a/solution.py
+++ b/solution.py
@@ -266,10 +266,10 @@
 
     @pl.when(first)
     def _():
-        for d in far:
+        for d in (5, 4, 3, 6, 2, 7, 1):
             x_copy(xwrap(d)).start()
+        for d in far + (0,):
             d_copy(xwrap(d)).start()
-        d_copy(x).start()
     for d in far:
         @pl.when((key_of(xwrap(d)) < key) & jnp.logical_not(first))
         def _(d=d):
@@ -556,9 +556,19 @@
 
     with jax.named_scope("ends"):
         less = jnp.where(z >= nz - 2, 2, jnp.where(z == nz - 3, 1, 0))
-        moved_some(fs, xs_sem, z - less + jnp.where(column & (z >= nz - 3), 1, 0))
+        lines = z - less + jnp.where(column & (z >= nz - 3), 1, 0)
         late = jnp.where(z >= nz - 2, 2 * NX, jnp.where(z == nz - 3, NX, 0))
-        moved_some(fs, xs_sem, late - jnp.where(plane & (z >= nz - 3), 1, 0))
+        lines = lines + late - jnp.where(plane & (z >= nz - 3), 1, 0)
+        totals = lax.div(nz + 1 - z, 4)
+        for slot, d, ok in raw:
+            totals = totals + jnp.where(ok, 1, 0)
+        for ref, n in ((fs, lines), (rw, totals)):
+            m = ref.shape[0]
+            while m > 0:
+                @pl.when(lax.rem(lax.div(n, m), 2) == 1)
+                def _(ref=ref, m=m):
+                    moved(ref.at[pl.ds(0, m)], xs_sem).wait()
+                m = m // 2
         moved(sx.at[pl.ds(0, NX - 1)], xs_sem).wait()
 
         @pl.when(row0)
@@ -572,14 +582,6 @@
         @pl.when(row1 & (x == 0))
         def _():
             moved(cb2.at[:, pl.ds(0, NX - 1)], xs_sem).wait()
-        for slot, d, ok in raw:
-            @pl.when(ok)
-            def _(slot=slot):
-                moved(rtot, xs_sem).wait()
-        for j in range(4):
-            @pl.when(z + 2 + 4 * j < nz)
-            def _(j=j):
-                moved(win, xs_sem).wait()
 
 
 def put(a_ref, b_ref, a_out, b_out, sem):

time: 54.6 us -> 54.7 us (level)
  no operation moved by 1% of the time
where the time goes in v8:
time: 54.7 us; the launch traced here: 54.6 us
  Pallas kernels  53.9 us (99%)
  between operations  0.64 us (1%)
    pallas_call x1, Pallas kernels, body(): pl.pallas_call(functools.partial(kernel, table, nz), out_shape=(pltpu.VME...  53.2 us

profile of v8, /device:TPU:66, one launch (start us, length us, event | category | flops | bytes accessed | tf_op | source)
XLA Modules:
  0.0 54.6 jit_solution(8431529128892891248)
XLA Ops:
  0.6 53.2 %retention.1 = (bf16[384,384]{1,0:T(8,128)(2,1)S(1)}, f32[3,1,128]{2,1,0:T(1,128)S(1)}) custom-call(bf16[384,384]{1,0:T(8,128)(2,1)} %q_hbm.1, bf16[384,384]{1,0:T(8,128)(2,1)} %k_hbm.1, bf16[384,384]{1,0:T(8,128)(2,1)} %v_hbm.1, bf16[384,384]{1,0:T(8,128)(2,1)} %g_hbm.1, f32[384]{0:T(512)} %gain_hbm.1), custom_call_target="tpu_custom_call" | custom-call | tf_op jit(solution)/shard_map/retention/pallas_call | solution.py:612
  53.8 0.7 %put.1 = (bf16[384,384]{1,0:T(8,128)(2,1)}, f32[3,1,128]{2,1,0:T(1,128)}) custom-call(bf16[384,384]{1,0:T(8,128)(2,1)S(1)} %get-tuple-element.6.a_ref, f32[3,1,128]{2,1,0:T(1,128)S(1)} %get-tuple-element.7.b_ref), custom_call_target="tpu_custom_call" | custom-call | tf_op jit(solution)/shard_map/put/pallas_call | solution.py:629

commit v9 on v8

--- a/solution.py
+++ b/solution.py
@@ -266,10 +266,10 @@
 
     @pl.when(first)
     def _():
-        for d in (5, 4, 3, 6, 2, 7, 1):
+        for d in far:
             x_copy(xwrap(d)).start()
-        for d in far + (0,):
             d_copy(xwrap(d)).start()
+        d_copy(x).start()
     for d in far:
         @pl.when((key_of(xwrap(d)) < key) & jnp.logical_not(first))
         def _(d=d):

time: 54.7 us -> 54.6 us (level)
  no operation moved by 1% of the time
where the time goes in v9:
time: 54.6 us; the launch traced here: 54.4 us
  Pallas kernels  53.8 us (99%)
  between operations  0.64 us (1%)
    pallas_call x1, Pallas kernels, body(): pl.pallas_call(functools.partial(kernel, table, nz), out_shape=(pltpu.VME...  53 us

profile of v9, /device:TPU:66, one launch (start us, length us, event | category | flops | bytes accessed | tf_op | source)
XLA Modules:
  0.0 54.4 jit_solution(957019043130919242)
XLA Ops:
  0.6 53.0 %retention.1 = (bf16[384,384]{1,0:T(8,128)(2,1)S(1)}, f32[3,1,128]{2,1,0:T(1,128)S(1)}) custom-call(bf16[384,384]{1,0:T(8,128)(2,1)} %q_hbm.1, bf16[384,384]{1,0:T(8,128)(2,1)} %k_hbm.1, bf16[384,384]{1,0:T(8,128)(2,1)} %v_hbm.1, bf16[384,384]{1,0:T(8,128)(2,1)} %g_hbm.1, f32[384]{0:T(512)} %gain_hbm.1), custom_call_target="tpu_custom_call" | custom-call | tf_op jit(solution)/shard_map/retention/pallas_call | solution.py:612
  53.7 0.7 %put.1 = (bf16[384,384]{1,0:T(8,128)(2,1)}, f32[3,1,128]{2,1,0:T(1,128)}) custom-call(bf16[384,384]{1,0:T(8,128)(2,1)S(1)} %get-tuple-element.6.a_ref, f32[3,1,128]{2,1,0:T(1,128)S(1)} %get-tuple-element.7.b_ref), custom_call_target="tpu_custom_call" | custom-call | tf_op jit(solution)/shard_map/put/pallas_call | solution.py:629

commit v10 on v7

--- a/solution.py
+++ b/solution.py
@@ -491,6 +491,13 @@
     def _():
         local_work()
 
+    ahead = (nz - 1 - z).astype(F32)
+    mine = []
+    for h in range(nh):
+        one = lds[h] * float(tokens * NX)
+        mine.append(jnp.exp((ahead + 1.0) * one) * cb[h, 0, pl.ds(z, 1), :]
+                    + jnp.exp(ahead * one) * rtot[h, pl.ds(z, 1), :])
+
     def outer_of(h):
         cols = pl.ds(h * DH, DH)
         lead = jnp.exp((r_iota(SUB) + 1.0) * lds[h])
@@ -523,12 +530,6 @@
     with jax.named_scope("norm"):
         norm_of(nh - 1)
 
-    ahead = (nz - 1 - z).astype(F32)
-    mine = []
-    for h in range(nh):
-        one = lds[h] * float(tokens * NX)
-        mine.append(jnp.exp((ahead + 1.0) * one) * cb[h, 0, pl.ds(z, 1), :]
-                    + jnp.exp(ahead * one) * rtot[h, pl.ds(z, 1), :])
     with jax.named_scope("fwait"):
         less = jnp.where(first, 0, jnp.where(z == 0, 3, jnp.where(z == 1, 2, 0)))
         moved_some(fr, fr_sem, nz - 1 - z - less)

time: 54.6 us -> 54.6 us (level)
  no operation moved by 1% of the time
where the time goes in v10:
time: 54.6 us; the launch traced here: 54.4 us
  Pallas kernels  53.8 us (99%)
  between operations  0.64 us (1%)
    pallas_call x1, Pallas kernels, body(): pl.pallas_call(functools.partial(kernel, table, nz), out_shape=(pltpu.VME...  53 us

profile of v10, /device:TPU:66, one launch (start us, length us, event | category | flops | bytes accessed | tf_op | source)
XLA Modules:
  0.0 54.4 jit_solution(4682357925375683376)
XLA Ops:
  0.6 53.0 %retention.1 = (bf16[384,384]{1,0:T(8,128)(2,1)S(1)}, f32[3,1,128]{2,1,0:T(1,128)S(1)}) custom-call(bf16[384,384]{1,0:T(8,128)(2,1)} %q_hbm.1, bf16[384,384]{1,0:T(8,128)(2,1)} %k_hbm.1, bf16[384,384]{1,0:T(8,128)(2,1)} %v_hbm.1, bf16[384,384]{1,0:T(8,128)(2,1)} %g_hbm.1, f32[384]{0:T(512)} %gain_hbm.1), custom_call_target="tpu_custom_call" | custom-call | tf_op jit(solution)/shard_map/retention/pallas_call | solution.py:611
  53.7 0.7 %put.1 = (bf16[384,384]{1,0:T(8,128)(2,1)}, f32[3,1,128]{2,1,0:T(1,128)}) custom-call(bf16[384,384]{1,0:T(8,128)(2,1)S(1)} %get-tuple-element.6.a_ref, f32[3,1,128]{2,1,0:T(1,128)S(1)} %get-tuple-element.7.b_ref), custom_call_target="tpu_custom_call" | custom-call | tf_op jit(solution)/shard_map/put/pallas_call | solution.py:628
